TPU v7x, 32 devices: a whole 2x2x4 slice. The times are simulated.
32 devices in a mesh: stn: 8 (over z, x), pts: 2 (over core), freq: 2 (over y).
Axes of the slice: x: 2, y: 2, z: 4, core: 2. Of those that a mesh axis runs over, the one named last changes fastest.
Arguments:
- greens: bfloat16 [2, 4, 2048, 4096], P(None, 'freq', 'stn', 'pts'), may hold values from -6 to 6
- noise_weights: bfloat16 [2, 4, 2048, 2048], P(None, 'freq', 'stn'), may hold values from -12 to 12, as said below
Outputs:
- kernel: float32 [4096], P('pts')
Inputs may be any that keep to these rules, and one draw needn't show every extreme that they name: For every frequency, noise_weights[0] is symmetric and noise_weights[1] antisymmetric in the two station dimensions, so each frequency's matrix is Hermitian.
All inputs are finite; a program needn't handle non-finite values. Where the computation divides by a largest or mean magnitude, that divisor is 1e-20 or more.
Results may differ from a plain program's by a relative error of at most 0.0003.
Values may be sent and summed in bfloat16 or wider, within the bound.
A program may use at most 192 MiB of HBM per device.

v0:
```python
import functools

import jax
import jax.numpy as jnp
from jax import lax
from jax.experimental import pallas as pl
from jax.experimental.pallas import tpu as pltpu
from jax.sharding import PartitionSpec as P

MESH = pl.DeviceIdType.MESH
LANES = 128


def remote(src, dst, send_sem, recv_sem, target):
    return pltpu.make_async_remote_copy(
        src_ref=src, dst_ref=dst, send_sem=send_sem, recv_sem=recv_sem,
        device_id=target, device_id_type=MESH,
    )


def ring_kernel(
    n, n_freq, h, stations, chunk, nq, blocked,
    greens, weights, out,
    g_own, g_pair, near, far, w_own, w_pair, acc, red, max_out, max_in,
    own_sem, w_own_sem, pair_send, pair_recv, wp_send, wp_recv, sib_sem,
    in_send, in_recv, out_send, far_recv, red_send, red_recv, max_sem, hello_sem, pair_hello,
):
    m = n // 2
    side_len = m // 2
    sub = chunk // LANES
    half_rows = h // 2
    me = lax.axis_index("stn")
    core = lax.axis_index("pts")
    fq = lax.axis_index("freq")
    parity = lax.rem(me, 2)
    z = me // 2
    hi = (z >= side_len).astype(jnp.int32)
    edge = jnp.where(hi == 1, m - 1 - z, z)
    inward = jnp.where(hi == 1, -2, 2)
    inner = edge == side_len - 1
    s_base = hi * nq
    r_base = (1 - hi) * nq
    pair_dev = {"stn": me + 1 - 2 * parity}
    in_dev = {"stn": me + inward}
    out_dev = {"stn": me - inward}
    n_far = side_len * 2 * nq
    n_near = edge * 4 * nq
    n_near_max = (side_len - 1) * 4 * nq
    steps = max(n_far, n_near_max, 3 * nq + 2)
    spread = side_len == 2
    catch_up = 2 * nq + 1 if spread else max((steps * 25) // 32, 3 * nq + 1)
    left = steps - catch_up
    per_step = -(-steps // (steps - catch_up))

    def columns(q):
        return pl.ds(pl.multiple_of(q * chunk, LANES), chunk)

    def w_src(freq, j, rows):
        if blocked:
            return weights.at[:, freq, j, rows, :]
        return weights.at[:, freq, rows, pl.ds(pl.multiple_of(j * h, LANES), h)]

    def global_block(e, opposite):
        low = jnp.where(opposite, 1 - hi, hi) == 0
        return jnp.where(low, e, m - 1 - e)

    def near_slot(receiver_edge, p, half, b, c):
        return ((p * 2 + half) * receiver_edge + (receiver_edge - 1 - b)) * nq + c

    def far_slot(p, b, c):
        return (p * side_len + (side_len - 1 - b)) * nq + c

    def send_inward(src, p, half, b, c):
        q = jnp.where(half == 0, s_base, r_base) + c

        if side_len > 1:
            @pl.when(jnp.logical_not(inner))
            def _():
                slot = near_slot(edge + 1, p, half, b, c)
                remote(src, near.at[b, p, q], in_send.at[slot], in_recv.at[slot], in_dev).start()

        @pl.when(jnp.logical_and(inner, half == 0))
        def _():
            slot = far_slot(p, b, c)
            remote(src, far.at[b, p, c], in_send.at[slot], far_recv.at[slot], in_dev).start()

    freq_dev = {"freq": n_freq - 1 - fq}
    barrier = pltpu.get_barrier_semaphore()
    up, down = z < m - 1, z > 0
    greeted = [pair_dev, {"pts": 1 - core}, freq_dev]

    def greet(sem, device):
        pl.semaphore_signal(sem, inc=1, device_id=device, device_id_type=MESH)

    def along_z(sem_down, sem_up):
        @pl.when(up)
        def _():
            greet(sem_up, {"stn": me + 2})

        @pl.when(down)
        def _():
            greet(sem_down, {"stn": me - 2})

    for device in greeted:
        greet(barrier, device)
    along_z(barrier, barrier)
    pl.semaphore_wait(barrier, len(greeted) + up.astype(jnp.int32) + down.astype(jnp.int32))

    def hello():
        @pl.loop(0, m - 1)
        def _(r):
            along_z(hello_sem.at[0, r], hello_sem.at[1, r])

            @pl.when(up)
            def _():
                pl.semaphore_wait(hello_sem.at[0, r], 1)

            @pl.when(down)
            def _():
                pl.semaphore_wait(hello_sem.at[1, r], 1)

        for i, device in enumerate((pair_dev, freq_dev)):
            greet(pair_hello.at[i], device)
            pl.semaphore_wait(pair_hello.at[i], 1)

    every_row = pl.ds(0, h)
    pair_rows = pl.ds(pl.multiple_of(core * half_rows, 8), half_rows)

    def pair_q(i):
        return jnp.where(i < nq, s_base + i, r_base + i - nq)

    def pair_copy(i):
        q = pair_q(i)
        return remote(
            greens.at[:, 1 - parity, :, columns(q)], g_pair.at[q],
            pair_send.at[i], pair_recv.at[i], pair_dev,
        )

    def w_pair_copy(j):
        return remote(
            w_src(1 - parity, j, pair_rows), w_pair.at[j, :, pair_rows, :],
            wp_send.at[j], wp_recv.at[j], pair_dev,
        )

    def sibling_copy(rows):
        return remote(
            w_pair.at[:, :, rows, :], w_pair.at[:, :, rows, :],
            sib_sem.at[0], sib_sem.at[1], {"pts": 1 - core},
        )

    def own_copy(q):
        return pltpu.make_async_copy(
            greens.at[:, parity, :, columns(q)], g_own.at[q], own_sem.at[q]
        )

    def w_own_copy(j):
        return pltpu.make_async_copy(w_src(parity, j, every_row), w_own.at[j], w_own_sem.at[j])

    @pl.loop(0, 2 * nq)
    def _(i):
        @pl.when(i < nq)
        def _():
            pair_copy(i).start()

        half = i // nq
        c = lax.rem(i, nq)
        send_inward(greens.at[:, parity, :, columns(pair_q(i))], 0, half, edge, c)
        own_copy(i).start()

    @pl.loop(0, n)
    def _(j):
        w_pair_copy(j).start()
        w_own_copy(j).start()

    @pl.loop(nq, 2 * nq)
    def _(i):
        pair_copy(i).start()

    hello()

    acc[...] = jnp.zeros_like(acc)

    @pl.loop(0, 2 * nq)
    def _(q):
        own_copy(q).wait()

    @pl.loop(0, n)
    def _(j):
        w_own_copy(j).wait()

    def contribute(w, gi, gj, q, weight):
        for s in range(sub):
            part = slice(s * LANES, (s + 1) * LANES)
            both = jnp.concatenate([gj[0, :, part], gj[1, :, part]], axis=1)
            ab = jnp.dot(w[...].reshape(2 * h, h), both, preferred_element_type=jnp.float32)
            a, b = ab[:h], ab[h:]
            t = gi[0, :, part].astype(jnp.float32) * (a[:, :LANES] - b[:, LANES:])
            t = t + gi[1, :, part].astype(jnp.float32) * (a[:, LANES:] + b[:, :LANES])
            t = jnp.sum(t.reshape(h // 8, 8, LANES), axis=0)
            acc[q * sub + s] += t * weight

    def far_at(t):
        p = t // (side_len * nq)
        rest = lax.rem(t, side_len * nq)
        return p, side_len - 1 - rest // nq, lax.rem(rest, nq)

    def near_at(t):
        width = jnp.maximum(edge, 1) * nq
        p = t // (2 * width)
        half = lax.rem(t // width, 2)
        rest = lax.rem(t, width)
        return p, half, jnp.maximum(edge, 1) - 1 - rest // nq, lax.rem(rest, nq)

    def part_of(p):
        return jnp.where(p == 0, parity, 1 - parity)

    def far_work(t, w, g):
        p, b, c = far_at(t)
        q = r_base + c
        j = global_block(b, True) * 2 + part_of(p)
        contribute(w.at[j], g.at[q], far.at[b, p, c], q, 2.0)

    def near_work(t, w, g):
        p, half, b, c = near_at(t)
        q = jnp.where(half == 0, s_base, r_base) + c
        j = global_block(b, False) * 2 + part_of(p)
        contribute(w.at[j], g.at[q], near.at[b, p, q], q, 2.0)

    def far_wait(t):
        p, b, c = far_at(t)
        ref = far.at[b, p, c]
        remote(ref, ref, out_send.at[t], far_recv.at[t], in_dev).wait_recv()

        @pl.when(edge > 0)
        def _():
            remote(ref, ref, out_send.at[t], far_recv.at[t], out_dev).start()

    def near_wait(t):
        p, half, b, c = near_at(t)
        q = jnp.where(half == 0, s_base, r_base) + c
        ref = near.at[b, p, q]
        remote(ref, ref, in_send.at[t], in_recv.at[t], out_dev).wait_recv()
        send_inward(ref, p, half, b, c)

    def newest(u):
        far_work(u, w_pair, g_pair)

        @pl.when(u < n_near)
        def _():
            near_work(u, w_pair, g_pair)

    @pl.loop(0, steps)
    def _(t):
        has_pair = jnp.logical_and(jnp.logical_and(t >= nq, t <= 3 * nq), t != 2 * nq)
        turn = t - nq - (t > 2 * nq).astype(jnp.int32)

        @pl.when(has_pair)
        def _():
            i = turn
            pair_copy(i).wait_recv()
            send_inward(g_pair.at[pair_q(i)], 1, i // nq, edge, lax.rem(i, nq))

        @pl.when(t < n_far)
        def _():
            far_wait(t)

        if side_len > 1:
            @pl.when(t < n_near)
            def _():
                near_wait(t)

        @pl.when(t == catch_up - 1)
        def _():
            @pl.loop(0, n)
            def _(j):
                w_pair_copy(j).wait_recv()

            sibling_copy(pair_rows).start()

        @pl.when(t < 2 * nq)
        def _():
            contribute(w_own.at[2 * z + parity], g_own.at[t], g_own.at[t], t, 1.0)

        @pl.when(has_pair)
        def _():
            q = pair_q(turn)
            contribute(w_own.at[2 * z + 1 - parity], g_own.at[q], g_pair.at[q], q, 2.0)

        @pl.when(t < n_far)
        def _():
            far_work(t, w_own, g_own)

        if side_len > 1:
            @pl.when(t < n_near)
            def _():
                near_work(t, w_own, g_own)

        @pl.when(t == catch_up)
        def _():
            sibling_copy(pl.ds(pl.multiple_of((1 - core) * half_rows, 8), half_rows)).wait_recv()

        @pl.when(t >= catch_up)
        def _():
            first = (t - catch_up) * per_step
            last = jnp.minimum(first + per_step, steps)
            if spread:
                first = ((t - catch_up) * 2 * nq) // left
                last = ((t - catch_up + 1) * 2 * nq) // left

            @pl.loop(first, last)
            def _(u):
                @pl.when(u < 2 * nq)
                def _():
                    q = pair_q(u)
                    contribute(w_pair.at[2 * z + 1 - parity], g_pair.at[q], g_pair.at[q], q, 1.0)

                if spread:
                    far_work(lax.rem(u, side_len) * nq + u // side_len, w_pair, g_pair)
                else:
                    @pl.when(u < n_far)
                    def _():
                        far_work(u, w_pair, g_pair)

                if side_len > 1:
                    @pl.when(u < n_near)
                    def _():
                        near_work(u, w_pair, g_pair)

            if spread:
                newest(t - 1)

    if spread:
        newest(steps - 1)

    total = n * n_freq
    rank = me * n_freq + fq
    red[rank] = jnp.sum(acc[...], axis=1) / stations

    def share_copy(k, source):
        target = lax.rem(rank + k, total)
        return remote(
            red.at[source], red.at[source], red_send.at[k - 1], red_recv.at[k - 1],
            {"stn": target // n_freq, "freq": lax.rem(target, n_freq)},
        )

    @pl.loop(1, total)
    def _(k):
        share_copy(k, rank).start()

    @pl.loop(1, total)
    def _(k):
        share_copy(k, lax.rem(rank - k + total, total)).wait_recv()

    raw = red[0]
    for d in range(1, total):
        raw = raw + red[d]
    max_out[...] = jnp.broadcast_to(jnp.max(jnp.abs(raw)), max_out.shape)
    max_copy = remote(max_out, max_in, max_sem.at[0], max_sem.at[1], {"pts": 1 - core})
    max_copy.start()

    @pl.loop(1, total)
    def _(k):
        share_copy(k, rank).wait_send()

    @pl.loop(0, 2 * nq)
    def _(i):
        pair_copy(i).wait_send()

    @pl.loop(0, n)
    def _(j):
        w_pair_copy(j).wait_send()

    sibling_copy(pair_rows).wait_send()
    ref = far.at[0, 0, 0]

    @pl.loop(0, jnp.where(inner, n_far, (edge + 1) * 4 * nq))
    def _(t):
        remote(ref, ref, in_send.at[t], far_recv.at[0], in_dev).wait_send()

    @pl.when(edge > 0)
    def _():
        @pl.loop(0, n_far)
        def _(t):
            remote(ref, ref, out_send.at[t], far_recv.at[0], out_dev).wait_send()

    max_copy.wait()
    largest = jnp.maximum(max_out[0:1, 0:1], max_in[0:1, 0:1])
    out[...] = raw / (largest + 1e-6)


def kernel_body(n, n_freq, greens, weights):
    _, _, h, points = greens.shape
    stations = weights.shape[3]
    half = points // 2
    chunk = LANES
    while chunk * 2 * h <= 32768 and half % (chunk * 2) == 0:
        chunk *= 2
    nq = half // chunk
    side_len = n // 4
    n_far = side_len * 2 * nq
    n_near = max(side_len - 1, 1) * 4 * nq
    blocked = h % LANES != 0
    if blocked:
        weights = weights.reshape(2, weights.shape[1], h, n, h).swapaxes(2, 3)
    dma = pltpu.SemaphoreType.DMA
    bf16, f32 = jnp.bfloat16, jnp.float32
    rows = points // LANES
    out = pl.pallas_call(
        functools.partial(ring_kernel, n, n_freq, h, stations, chunk, nq, blocked),
        out_shape=jax.ShapeDtypeStruct((rows, LANES), f32),
        in_specs=[pl.BlockSpec(memory_space=pl.ANY)] * 2,
        out_specs=pl.BlockSpec(memory_space=pltpu.VMEM),
        scratch_shapes=[
            pltpu.VMEM((2 * nq, 2, h, chunk), bf16),
            pltpu.VMEM((2 * nq, 2, h, chunk), bf16),
            pltpu.VMEM((max(side_len - 1, 1), 2, 2 * nq, 2, h, chunk), bf16),
            pltpu.VMEM((side_len, 2, nq, 2, h, chunk), bf16),
            pltpu.VMEM((n, 2, h, h), bf16),
            pltpu.VMEM((n, 2, h, h), bf16),
            pltpu.VMEM((rows, 8, LANES), f32),
            pltpu.VMEM((n * n_freq, rows, LANES), f32),
            pltpu.VMEM((8, LANES), f32),
            pltpu.VMEM((8, LANES), f32),
            dma((2 * nq,)), dma((n,)), dma((2 * nq,)), dma((2 * nq,)), dma((n,)), dma((n,)), dma((2,)),
            dma((max(n_near, n_far),)), dma((n_near,)), dma((n_far,)), dma((n_far,)),
            dma((n * n_freq - 1,)), dma((n * n_freq - 1,)), dma((2,)),
            pltpu.SemaphoreType.REGULAR((2, n // 2 - 1)), pltpu.SemaphoreType.REGULAR((2,)),
        ],
        compiler_params=pltpu.CompilerParams(
            collective_id=0, has_side_effects=True, vmem_limit_bytes=60 * 1024 * 1024
        ),
    )(greens, weights)
    return out.reshape(points)


def passed_along(x, axis, by):
    size = lax.axis_size(axis)
    return lax.ppermute(x, axis, [(i, (i + by) % size) for i in range(size)])


def mixing_of(weights):
    negated = -weights[1]
    return jnp.stack([jnp.stack([weights[0], negated]), jnp.stack([weights[1], weights[0]])])


def body(greens, noise_weights):
    station_rows = greens.shape[2]
    stations = noise_weights.shape[3]
    device_index = lax.axis_index("stn")
    cycle_length = lax.axis_size("stn")
    mixing = mixing_of(noise_weights)

    def block_product(columns_start, arriving):
        block_rows = arriving.shape[2]
        weights_block = lax.dynamic_slice_in_dim(mixing, columns_start, block_rows, 4)
        return jnp.einsum(
            "ocfin,cfnx->ofix", weights_block, arriving, preferred_element_type=jnp.float32
        )

    half_way = cycle_length // 2
    diagonal = block_product(device_index * station_rows, greens)

    def advance(offset, loop_state):
        running, current = loop_state
        current = passed_along(current, "stn", -1)
        source = (device_index + offset) % cycle_length
        weight = jnp.where(offset == half_way, 1.0, 2.0).astype(jnp.float32)
        running = running + weight * block_product(source * station_rows, current)
        return (running, current)

    summed, current = lax.fori_loop(1, half_way + 1, advance, (diagonal, greens))
    green_real = greens[0].astype(jnp.float32)
    green_imag = greens[1].astype(jnp.float32)
    partial_kernel = (
        jnp.sum(green_real * summed[0] + green_imag * summed[1], axis=(0, 1)) / stations
    )
    raw_kernel = lax.psum(partial_kernel, "stn")
    raw_kernel = lax.psum(raw_kernel, "freq")
    largest = lax.pmax(jnp.max(jnp.abs(raw_kernel)), "pts")
    return raw_kernel / (largest + 1e-06)


def solution(mesh):
    n, cores, n_freq = mesh.shape["stn"], mesh.shape["pts"], mesh.shape["freq"]

    def either(greens, noise_weights):
        _, freqs, rows, points = greens.shape
        fits = n % 4 == 0 and cores == 2 and freqs == 2 and n_freq == 2 and rows % 32 == 0 and points % (2 * LANES) == 0
        if fits:
            return kernel_body(n, n_freq, greens, noise_weights)
        return body(greens, noise_weights)

    in_specs = (P(None, "freq", "stn", "pts"), P(None, "freq", "stn", None))
    return jax.shard_map(either, mesh=mesh, in_specs=in_specs, out_specs=P("pts"), check_vma=False)
```

profile of v0, /device:TPU:0, one launch (start us, length us, event | category | flops | bytes accessed | tf_op | source)
XLA Modules:
  0.0 113.2 jit_solution(8051481320211434854)
XLA Ops:
  0.0 111.9 %shard_map.28 = f32[16,128]{1,0:T(8,128)} custom-call(bf16[2,2,256,2048]{3,2,1,0:T(8,128)(2,1)} %greens.1, bf16[2,2,256,2048]{3,2,1,0:T(8,128)(2,1)} %weights.1), custom_call_target="tpu_custom_call" | custom-call | tf_op jit(solution)/shard_map/pallas_call | solution.py:408
  111.9 1.3 %copy.4 = f32[2048]{0:T(1024)} copy(f32[2048]{0:T(1024)} %bitcast.1) | data formatting | bytes 16384
where the time goes:
time: 113 us
  Pallas kernels  112 us (99%)
  local copies, waits for them, and re-layouts  1.3 us (1%)
    pallas_call x1, Pallas kernels, kernel_body(): pl.pallas_call(functools.partial(ring_kernel, n, n_freq, h, stations, chu...  112 us

commit v1 on v0

--- a/solution.py
+++ b/solution.py
@@ -402,6 +402,8 @@
     blocked = h % LANES != 0
     if blocked:
         weights = weights.reshape(2, weights.shape[1], h, n, h).swapaxes(2, 3)
+    if side_len == 2 and nq >= 4:
+        return line_body(n_freq, chunk, nq, blocked, greens, weights)
     dma = pltpu.SemaphoreType.DMA
     bf16, f32 = jnp.bfloat16, jnp.float32
     rows = points // LANES
@@ -433,6 +435,627 @@
     return out.reshape(points)
 
 
+def line_kernel(
+    n_freq, h, stations, chunk, nq, kept, late, blocked,
+    greens, weights, out,
+    g_own, g_pair, near, far, w_own, w_pair, w_edge, acc, part, side, extra, extras, max_out, max_in,
+    own_sem, w_own_sem, pair_send, pair_recv, wp_send, wp_recv, sib_sem, we_send, we_recv, we_sib,
+    in_send, near_recv, far_recv, down_send, back_send, part_send, part_recv, side_sem,
+    extra_send, extra_recv, max_sem, hello_sem, pair_hello,
+):
+    n = 8
+    sub = chunk // LANES
+    half_rows = h // 2
+    steps = 4 * nq
+    me = lax.axis_index("stn")
+    core = lax.axis_index("pts")
+    fq = lax.axis_index("freq")
+    parity = lax.rem(me, 2)
+    z = me // 2
+    hi = z // 2
+    inner = jnp.logical_or(z == 1, z == 2)
+    outer = jnp.logical_not(inner)
+    s_base = hi * nq
+    r_base = (1 - hi) * nq
+    rank = me * n_freq + fq
+    total = n * n_freq
+    inward = jnp.where(hi == 1, -2, 2)
+    pair_dev = {"stn": me + 1 - 2 * parity}
+    in_dev = {"stn": me + inward}
+    out_dev = {"stn": me - inward}
+    core_dev = {"pts": 1 - core}
+    freq_dev = {"freq": n_freq - 1 - fq}
+    across_dev = {"stn": lax.rem(me + n // 2, n)}
+    other_inner = 2 - hi
+    other_edge = 3 - 3 * hi
+    near_z = jnp.where(inner, z - inward // 2, z + inward // 2)
+
+    def columns(q):
+        return pl.ds(pl.multiple_of(q * chunk, LANES), chunk)
+
+    def w_src(freq, j, rows):
+        if blocked:
+            return weights.at[:, freq, j, rows, :]
+        return weights.at[:, freq, rows, pl.ds(pl.multiple_of(j * h, LANES), h)]
+
+    def block_of(where, p):
+        return 2 * where + jnp.where(p == 0, parity, 1 - parity)
+
+    def far_block(e):
+        return block_of(jnp.where(lax.rem(e, 2) == 0, other_inner, other_edge), e // 2)
+
+    last_block = block_of(other_edge, 1)
+    every_row = pl.ds(0, h)
+    my_rows = pl.ds(pl.multiple_of(core * half_rows, 8), half_rows)
+    sib_rows = pl.ds(pl.multiple_of((1 - core) * half_rows, 8), half_rows)
+
+    def pair_q(i):
+        return jnp.where(i < nq, s_base + i, r_base + i - nq)
+
+    def own_copy(q):
+        return pltpu.make_async_copy(
+            greens.at[:, parity, :, columns(q)], g_own.at[q], own_sem.at[q]
+        )
+
+    def w_own_copy(j):
+        return pltpu.make_async_copy(w_src(parity, j, every_row), w_own.at[j], w_own_sem.at[j])
+
+    def pair_copy(i):
+        q = pair_q(i)
+        return remote(
+            greens.at[:, 1 - parity, :, columns(q)], g_pair.at[q],
+            pair_send.at[i], pair_recv.at[i], pair_dev,
+        )
+
+    def w_pair_copy(j):
+        return remote(
+            w_src(1 - parity, j, my_rows), w_pair.at[j, :, my_rows, :],
+            wp_send.at[j], wp_recv.at[j], pair_dev,
+        )
+
+    def sibling_copy(rows):
+        part_of_w = w_pair.at[:, :, rows, :]
+        return remote(part_of_w, part_of_w, sib_sem.at[0], sib_sem.at[1], core_dev)
+
+    def edge_sibling_copy(rows):
+        part_of_w = w_edge.at[:, :, rows, :]
+        return remote(part_of_w, part_of_w, we_sib.at[0], we_sib.at[1], core_dev)
+
+    def up_copy(src, p, i):
+        slot = p * 2 * nq + i
+        return remote(src, near.at[p, pair_q(i)], in_send.at[slot], near_recv.at[slot], in_dev)
+
+    def up_weights(src, p):
+        return remote(src, w_edge.at[p, :, my_rows, :], we_send.at[p], we_recv.at[p], in_dev)
+
+    def mid_copy(src, slot):
+        return remote(src, far.at[slot], in_send.at[slot], far_recv.at[slot], in_dev)
+
+    def down_copy(slot):
+        return remote(far.at[slot], far.at[slot], down_send.at[slot], far_recv.at[slot], out_dev)
+
+    def back_copy(src, p, c):
+        return remote(
+            src, near.at[p, (1 - hi) * nq + c], back_send.at[p * kept + c],
+            near_recv.at[p * 2 * nq + nq + c], out_dev,
+        )
+
+    @pl.loop(0, 2 * nq)
+    def _(i):
+        own_copy(pair_q(i)).start()
+
+    @pl.loop(0, n)
+    def _(j):
+        w_own_copy(j).start()
+
+    barrier = pltpu.get_barrier_semaphore()
+    up, down = z < 3, z > 0
+    greeted = [pair_dev, core_dev, freq_dev]
+
+    def greet(sem, device):
+        pl.semaphore_signal(sem, inc=1, device_id=device, device_id_type=MESH)
+
+    def along_z(sem_down, sem_up):
+        @pl.when(up)
+        def _():
+            greet(sem_up, {"stn": me + 2})
+
+        @pl.when(down)
+        def _():
+            greet(sem_down, {"stn": me - 2})
+
+    along_z(barrier, barrier)
+    for device in greeted:
+        greet(barrier, device)
+    pl.semaphore_wait(barrier, len(greeted) + up.astype(jnp.int32) + down.astype(jnp.int32))
+
+    @pl.loop(0, nq)
+    def _(i):
+        q = pair_q(i)
+        own_copy(q).wait()
+
+        @pl.when(inner)
+        def _():
+            mid_copy(g_own.at[q], i).start()
+
+        @pl.when(outer)
+        def _():
+            up_copy(g_own.at[q], 0, i).start()
+
+        @pl.when(i < n)
+        def _():
+            w_pair_copy(i).start()
+
+    for j in range(nq, n):
+        w_pair_copy(j).start()
+
+    @pl.loop(0, 2 * nq)
+    def _(i):
+        pair_copy(i).start()
+
+    @pl.loop(nq, 2 * nq)
+    def _(i):
+        q = pair_q(i)
+        own_copy(q).wait()
+
+        @pl.when(jnp.logical_and(inner, i < nq + kept))
+        def _():
+            back_copy(g_own.at[q], 0, i - nq).start()
+
+        @pl.when(jnp.logical_and(outer, i >= nq + kept))
+        def _():
+            up_copy(g_own.at[q], 0, i).start()
+
+    @pl.loop(0, n)
+    def _(j):
+        w_own_copy(j).wait()
+
+    @pl.when(outer)
+    def _():
+        up_weights(w_own.at[last_block, :, my_rows, :], 0).start()
+
+    @pl.loop(0, 3)
+    def _(r):
+        along_z(hello_sem.at[0, r], hello_sem.at[1, r])
+
+        @pl.when(up)
+        def _():
+            pl.semaphore_wait(hello_sem.at[0, r], 1)
+
+        @pl.when(down)
+        def _():
+            pl.semaphore_wait(hello_sem.at[1, r], 1)
+
+    for i, device in enumerate((pair_dev, freq_dev)):
+        greet(pair_hello.at[i], device)
+        pl.semaphore_wait(pair_hello.at[i], 1)
+
+    acc[...] = jnp.zeros_like(acc)
+
+    def contribute(w, gi, gj, q, weight):
+        for s in range(sub):
+            lanes = slice(s * LANES, (s + 1) * LANES)
+            both = jnp.concatenate([gj[0, :, lanes], gj[1, :, lanes]], axis=1)
+            ab = jnp.dot(w[...].reshape(2 * h, h), both, preferred_element_type=jnp.float32)
+            a, b = ab[:h], ab[h:]
+            t = gi[0, :, lanes].astype(jnp.float32) * (a[:, :LANES] - b[:, LANES:])
+            t = t + gi[1, :, lanes].astype(jnp.float32) * (a[:, LANES:] + b[:, :LANES])
+            t = jnp.sum(t.reshape(h // 8, 8, LANES), axis=0)
+            acc[q * sub + s] += t * weight
+
+    own_pair_block = block_of(z, 1)
+
+    def own_work(q):
+        contribute(w_own.at[me], g_own.at[q], g_own.at[q], q, 1.0)
+
+    def cross_work(q):
+        contribute(w_own.at[own_pair_block], g_own.at[q], g_pair.at[q], q, 2.0)
+
+    def pair_work(q):
+        contribute(w_pair.at[own_pair_block], g_pair.at[q], g_pair.at[q], q, 1.0)
+
+    def far_work(slot, w, g):
+        q = r_base + lax.rem(slot, nq)
+        contribute(w.at[far_block(slot // nq)], g.at[q], far.at[slot], q, 2.0)
+
+    def near_work(p, q, w, g):
+        contribute(w.at[block_of(near_z, p)], g.at[q], near.at[p, q], q, 2.0)
+
+    def edge_work(c):
+        q = r_base + c
+
+        @pl.loop(0, 2)
+        def _(p):
+            contribute(w_edge.at[p], near.at[p, q], far.at[3 * nq + c], q, 2.0)
+
+    def wait_far(t):
+        ref = far.at[t]
+        remote(ref, ref, down_send.at[t], far_recv.at[t], in_dev).wait_recv()
+
+    def wait_near(p, i):
+        slot = p * 2 * nq + i
+        ref = near.at[p, pair_q(i)]
+        remote(ref, ref, in_send.at[slot], near_recv.at[slot], in_dev).wait_recv()
+
+    def wait_w_pair():
+        @pl.loop(0, n)
+        def _(j):
+            w_pair_copy(j).wait_recv()
+
+        sibling_copy(my_rows).start()
+
+    def share_part():
+        part[rank] = jnp.sum(acc[...], axis=1) / stations
+
+        @pl.loop(0, total // 2 - 1)
+        def _(k):
+            part_copy(total // 2 - 1 - k, rank).start()
+
+    def at_rank(target):
+        return {"stn": target // n_freq, "freq": lax.rem(target, n_freq)}
+
+    def flipped(k):
+        bit, flip = total // 2, jnp.int32(0)
+        while bit:
+            mine = lax.rem(rank // bit, 2)
+            turn = lax.rem(k // bit, 2)
+            flip = flip + bit * (mine + turn - 2 * mine * turn)
+            bit //= 2
+        return flip
+
+    def part_copy(k, source):
+        ref = part.at[source]
+        return remote(ref, ref, part_send.at[k - 1], part_recv.at[k - 1], at_rank(flipped(k)))
+
+    near_second = 2 * nq - kept + 1
+    near_third = 3 * nq - kept + 2
+    near_end = 4 * nq - 2 * kept + 2
+
+    def near_at(t):
+        second = t >= near_second
+        third = t >= near_third
+        i = jnp.where(t < nq, t, t + kept)
+        i = jnp.where(second, t - near_second, i)
+        i = jnp.where(third, t - near_third + nq + kept, i)
+        present = jnp.logical_and(t != near_second - 1, t != near_third - 1)
+        return jnp.logical_and(present, t < near_end), second.astype(jnp.int32), i
+
+    @pl.when(inner)
+    def _():
+        @pl.loop(0, steps)
+        def _(t):
+            has_near, p, i = near_at(t)
+            has_pair = jnp.logical_and(t >= nq, t < 3 * nq)
+            turn = t - nq
+            wait_far(t)
+
+            @pl.when(t < 3 * nq + kept)
+            def _():
+                down_copy(t).start()
+
+            @pl.when(has_near)
+            def _():
+                wait_near(p, i)
+
+                @pl.when(i < nq)
+                def _():
+                    mid_copy(near.at[p, pair_q(i)], (2 * p + 1) * nq + i).start()
+
+            @pl.when(t == nq)
+            def _():
+                wait_w_pair()
+
+            @pl.when(has_pair)
+            def _():
+                pair_copy(turn).wait_recv()
+
+                @pl.when(turn < nq)
+                def _():
+                    mid_copy(g_pair.at[pair_q(turn)], 2 * nq + turn).start()
+
+                @pl.when(jnp.logical_and(turn >= nq, turn < nq + kept))
+                def _():
+                    back_copy(g_pair.at[pair_q(turn)], 1, turn - nq).start()
+
+            @pl.when(t == nq + 2)
+            def _():
+                sibling_copy(sib_rows).wait_recv()
+
+            @pl.when(t == 3 * nq + kept - 1)
+            def _():
+                for r in range(2):
+                    up_weights(w_edge.at[r, :, my_rows, :], r).wait_recv()
+                edge_sibling_copy(my_rows).start()
+
+            @pl.when(t == 3 * nq + kept)
+            def _():
+                edge_sibling_copy(sib_rows).wait_recv()
+
+            far_work(t, w_own, g_own)
+
+            @pl.when(t < 2 * nq)
+            def _():
+                own_work(t)
+
+            @pl.when(has_near)
+            def _():
+                q = pair_q(i)
+                near_work(p, q, w_own, g_own)
+
+                @pl.when(p == 1)
+                def _():
+                    near_work(p, q, w_pair, g_pair)
+
+            @pl.when(has_pair)
+            def _():
+                cross_work(pair_q(turn))
+
+            lag = t - nq - 2
+
+            @pl.when(jnp.logical_and(lag >= 0, lag < 2 * nq))
+            def _():
+                pair_work(pair_q(lag))
+
+                @pl.when(lag < nq)
+                def _():
+                    near_work(0, pair_q(lag), w_pair, g_pair)
+
+            @pl.when(jnp.logical_and(t >= 2 * nq, t < 3 * nq))
+            def _():
+                @pl.loop(0, 3)
+                def _(e):
+                    far_work(e * nq + t - 2 * nq, w_pair, g_pair)
+
+                @pl.when(t >= 2 * nq + kept)
+                def _():
+                    near_work(0, r_base + t - 2 * nq, w_pair, g_pair)
+
+            @pl.when(t >= 3 * nq)
+            def _():
+                far_work(t, w_pair, g_pair)
+
+            @pl.when(t >= 3 * nq + kept)
+            def _():
+                edge_work(t - 3 * nq)
+
+            @pl.when(t == steps - late - 1)
+            def _():
+                share_part()
+
+                @pl.loop((nq - late) * sub, nq * sub)
+                def _(c):
+                    acc[r_base * sub + c] = jnp.zeros((8, LANES), jnp.float32)
+
+    @pl.when(outer)
+    def _():
+        @pl.loop(0, 3 * nq + kept)
+        def _(t):
+            turn = t - nq + 2
+            has_pair = jnp.logical_and(turn >= 0, turn < 2 * nq)
+            back = t - 2 * nq - 4
+
+            @pl.when(turn == 0)
+            def _():
+                wait_w_pair()
+
+            @pl.when(has_pair)
+            def _():
+                pair_copy(turn).wait_recv()
+
+                @pl.when(jnp.logical_or(turn < nq, turn >= nq + kept))
+                def _():
+                    up_copy(g_pair.at[pair_q(turn)], 1, turn).start()
+
+                @pl.when(turn == nq - 1)
+                def _():
+                    up_weights(w_pair.at[last_block, :, my_rows, :], 1).start()
+
+            @pl.when(t == nq)
+            def _():
+                sibling_copy(sib_rows).wait_recv()
+
+            @pl.when(t < kept)
+            def _():
+                wait_near(0, nq + t)
+
+            @pl.when(jnp.logical_and(back >= 0, back < kept))
+            def _():
+                wait_near(1, nq + back)
+
+            wait_far(t)
+            far_work(t, w_own, g_own)
+
+            @pl.when(t < 2 * nq)
+            def _():
+                own_work(t)
+
+            @pl.when(t < kept)
+            def _():
+                near_work(0, r_base + t, w_own, g_own)
+
+            @pl.when(jnp.logical_and(back >= 0, back < kept))
+            def _():
+                q = r_base + back
+                near_work(0, q, w_pair, g_pair)
+                near_work(1, q, w_own, g_own)
+                near_work(1, q, w_pair, g_pair)
+
+            @pl.when(has_pair)
+            def _():
+                cross_work(pair_q(turn))
+
+            @pl.when(jnp.logical_and(t >= nq, t < 3 * nq))
+            def _():
+                pair_work(pair_q(t - nq))
+
+            @pl.when(jnp.logical_and(t >= 2 * nq, t < 3 * nq))
+            def _():
+                @pl.loop(0, 3)
+                def _(e):
+                    far_work(e * nq + t - 2 * nq, w_pair, g_pair)
+
+            @pl.when(t >= 3 * nq)
+            def _():
+                far_work(t, w_pair, g_pair)
+
+        share_part()
+
+    my_group = hi * 2 * n_freq + parity * n_freq + fq
+    late_rows = late * sub
+
+    def extra_copy(k, group):
+        ref = extras.at[group]
+        return remote(
+            extras.at[my_group], ref, extra_send.at[k - 1], extra_recv.at[group],
+            at_rank(flipped(k)),
+        )
+
+    @pl.when(inner)
+    def _():
+        for c in range(late_rows):
+            row = jnp.sum(acc[(r_base + nq - late) * sub + c], axis=0, keepdims=True) / stations
+            extras[my_group, c] = row
+
+        @pl.loop(0, total - 1)
+        def _(k):
+            extra_copy(total - 1 - k, my_group).start()
+
+    @pl.loop(1, total // 2)
+    def _(k):
+        part_copy(k, flipped(k)).wait_recv()
+
+    base = hi * (total // 2)
+    mine = part[base]
+    for d in range(1, total // 2):
+        mine = mine + part[base + d]
+    side[hi] = mine
+
+    def side_copy(which):
+        ref = side.at[which]
+        return remote(ref, ref, side_sem.at[0], side_sem.at[1], across_dev)
+
+    side_copy(hi).start()
+    side_copy(1 - hi).wait_recv()
+    extra[...] = side[0] + side[1]
+
+    @pl.loop(0, 4 * n_freq)
+    def _(g):
+        @pl.when(jnp.logical_or(outer, g != my_group))
+        def _():
+            ref = extras.at[g]
+            remote(ref, ref, extra_send.at[0], extra_recv.at[g], pair_dev).wait_recv()
+
+    for low in range(2):
+        for c in range(late_rows):
+            row = extras[low * 2 * n_freq, c]
+            for g in range(1, 2 * n_freq):
+                row = row + extras[low * 2 * n_freq + g, c]
+            at = ((1 - low) * nq + nq - late) * sub + c
+            extra[at:at + 1, :] += row
+
+    raw = extra[...]
+    max_out[...] = jnp.broadcast_to(jnp.max(jnp.abs(raw)), max_out.shape)
+    max_copy = remote(max_out, max_in, max_sem.at[0], max_sem.at[1], core_dev)
+    max_copy.start()
+
+    @pl.loop(0, 2 * nq)
+    def _(i):
+        pair_copy(i).wait_send()
+
+    @pl.loop(0, n)
+    def _(j):
+        w_pair_copy(j).wait_send()
+
+    sibling_copy(my_rows).wait_send()
+    side_copy(hi).wait_send()
+
+    @pl.loop(1, total // 2)
+    def _(k):
+        part_copy(k, rank).wait_send()
+
+    @pl.when(inner)
+    def _():
+        @pl.loop(0, steps)
+        def _(t):
+            mid_copy(far.at[t], t).wait_send()
+
+            @pl.when(t < 3 * nq + kept)
+            def _():
+                down_copy(t).wait_send()
+
+        @pl.loop(0, 2 * kept)
+        def _(i):
+            back_copy(g_own.at[0], i // kept, lax.rem(i, kept)).wait_send()
+
+        @pl.loop(1, total)
+        def _(k):
+            extra_copy(k, my_group).wait_send()
+
+        edge_sibling_copy(my_rows).wait_send()
+
+    @pl.when(outer)
+    def _():
+        @pl.loop(0, 4 * nq)
+        def _(s):
+            i = lax.rem(s, 2 * nq)
+
+            @pl.when(jnp.logical_or(i < nq, i >= nq + kept))
+            def _():
+                up_copy(g_own.at[0], s // (2 * nq), i).wait_send()
+
+        for r in range(2):
+            up_weights(w_edge.at[r, :, my_rows, :], r).wait_send()
+
+    max_copy.wait()
+    largest = jnp.maximum(max_out[0:1, 0:1], max_in[0:1, 0:1])
+    out[...] = raw / (largest + 1e-6)
+
+
+def line_body(n_freq, chunk, nq, blocked, greens, weights):
+    _, _, h, points = greens.shape
+    n = 8
+    kept, late = nq // 4, 3
+    stations = n * h
+    dma = pltpu.SemaphoreType.DMA
+    regular = pltpu.SemaphoreType.REGULAR
+    bf16, f32 = jnp.bfloat16, jnp.float32
+    rows = points // LANES
+    late_rows = late * (chunk // LANES)
+    total = n * n_freq
+    out = pl.pallas_call(
+        functools.partial(line_kernel, n_freq, h, stations, chunk, nq, kept, late, blocked),
+        out_shape=jax.ShapeDtypeStruct((rows, LANES), f32),
+        in_specs=[pl.BlockSpec(memory_space=pl.ANY)] * 2,
+        out_specs=pl.BlockSpec(memory_space=pltpu.VMEM),
+        scratch_shapes=[
+            pltpu.VMEM((2 * nq, 2, h, chunk), bf16),
+            pltpu.VMEM((2 * nq, 2, h, chunk), bf16),
+            pltpu.VMEM((2, 2 * nq, 2, h, chunk), bf16),
+            pltpu.VMEM((4 * nq, 2, h, chunk), bf16),
+            pltpu.VMEM((n, 2, h, h), bf16),
+            pltpu.VMEM((n, 2, h, h), bf16),
+            pltpu.VMEM((2, 2, h, h), bf16),
+            pltpu.VMEM((rows, 8, LANES), f32),
+            pltpu.VMEM((total, rows, LANES), f32),
+            pltpu.VMEM((2, rows, LANES), f32),
+            pltpu.VMEM((rows, LANES), f32),
+            pltpu.VMEM((4 * n_freq, late_rows, 1, LANES), f32),
+            pltpu.VMEM((8, LANES), f32),
+            pltpu.VMEM((8, LANES), f32),
+            dma((2 * nq,)), dma((n,)), dma((2 * nq,)), dma((2 * nq,)), dma((n,)), dma((n,)), dma((2,)),
+            dma((2,)), dma((2,)), dma((2,)),
+            dma((4 * nq,)), dma((4 * nq,)), dma((4 * nq,)), dma((4 * nq,)), dma((2 * kept,)),
+            dma((total // 2 - 1,)), dma((total // 2 - 1,)), dma((2,)),
+            dma((total - 1,)), dma((4 * n_freq,)), dma((2,)),
+            regular((2, 3)), regular((2,)),
+        ],
+        compiler_params=pltpu.CompilerParams(
+            collective_id=0, has_side_effects=True, vmem_limit_bytes=60 * 1024 * 1024
+        ),
+    )(greens, weights)
+    return out.reshape(points)
+
+
 def passed_along(x, axis, by):
     size = lax.axis_size(axis)
     return lax.ppermute(x, axis, [(i, (i + by) % size) for i in range(size)])

time: 113 us -> 107 us (0.947)
  Pallas kernels: 112 us -> 106 us
    pallas_call x1, Pallas kernels: 112 us -> 106 us  [line_body(): pl.pallas_call(functools.partial(line_kernel, n_freq, h, stations, chunk,...]
where the time goes in v1:
time: 107 us
  Pallas kernels  106 us (99%)
  local copies, waits for them, and re-layouts  1.3 us (1%)
    pallas_call x1, Pallas kernels, line_body(): pl.pallas_call(functools.partial(line_kernel, n_freq, h, stations, chunk,...  106 us

profile of v1, /device:TPU:0, one launch (start us, length us, event | category | flops | bytes accessed | tf_op | source)
XLA Modules:
  0.0 106.9 jit_solution(16823417014804459515)
XLA Ops:
  0.0 105.6 %shard_map.28 = f32[16,128]{1,0:T(8,128)} custom-call(bf16[2,2,256,2048]{3,2,1,0:T(8,128)(2,1)} %greens.1, bf16[2,2,256,2048]{3,2,1,0:T(8,128)(2,1)} %weights.1), custom_call_target="tpu_custom_call" | custom-call | tf_op jit(solution)/shard_map/pallas_call | solution.py:1025
  105.6 1.3 %copy.4 = f32[2048]{0:T(1024)} copy(f32[2048]{0:T(1024)} %bitcast.1) | data formatting | bytes 16384

commit v2 on v1

--- a/solution.py
+++ b/solution.py
@@ -435,6 +435,9 @@
     return out.reshape(points)
 
 
+FAR_FIRST = (11, 9, 10, 8, 15, 7, 13, 14, 5, 6, 12, 4, 3, 1, 2)
+
+
 def line_kernel(
     n_freq, h, stations, chunk, nq, kept, late, blocked,
     greens, weights, out,
@@ -492,10 +495,11 @@
     def pair_q(i):
         return jnp.where(i < nq, s_base + i, r_base + i - nq)
 
+    def g_src(q):
+        return greens.at[:, parity, :, columns(q)]
+
     def own_copy(q):
-        return pltpu.make_async_copy(
-            greens.at[:, parity, :, columns(q)], g_own.at[q], own_sem.at[q]
-        )
+        return pltpu.make_async_copy(g_src(q), g_own.at[q], own_sem.at[q])
 
     def w_own_copy(j):
         return pltpu.make_async_copy(w_src(parity, j, every_row), w_own.at[j], w_own_sem.at[j])
@@ -540,14 +544,6 @@
             near_recv.at[p * 2 * nq + nq + c], out_dev,
         )
 
-    @pl.loop(0, 2 * nq)
-    def _(i):
-        own_copy(pair_q(i)).start()
-
-    @pl.loop(0, n)
-    def _(j):
-        w_own_copy(j).start()
-
     barrier = pltpu.get_barrier_semaphore()
     up, down = z < 3, z > 0
     greeted = [pair_dev, core_dev, freq_dev]
@@ -571,77 +567,80 @@
 
     @pl.loop(0, nq)
     def _(i):
-        q = pair_q(i)
-        own_copy(q).wait()
+        src = g_src(pair_q(i))
 
         @pl.when(inner)
         def _():
-            mid_copy(g_own.at[q], i).start()
+            mid_copy(src, i).start()
 
         @pl.when(outer)
         def _():
-            up_copy(g_own.at[q], 0, i).start()
-
-        @pl.when(i < n)
-        def _():
-            w_pair_copy(i).start()
-
-    for j in range(nq, n):
+            up_copy(src, 0, i).start()
+
+    @pl.loop(0, n)
+    def _(j):
         w_pair_copy(j).start()
+        w_own_copy(j).start()
 
     @pl.loop(0, 2 * nq)
     def _(i):
+        own_copy(pair_q(i)).start()
         pair_copy(i).start()
 
     @pl.loop(nq, 2 * nq)
     def _(i):
-        q = pair_q(i)
+        src = g_src(pair_q(i))
+
+        @pl.when(jnp.logical_and(inner, i < nq + kept))
+        def _():
+            back_copy(src, 0, i - nq).start()
+
+        @pl.when(jnp.logical_and(outer, i >= nq + kept))
+        def _():
+            up_copy(src, 0, i).start()
+
+    @pl.when(outer)
+    def _():
+        up_weights(w_src(parity, last_block, my_rows), 0).start()
+
+    @pl.loop(0, 3)
+    def _(r):
+        along_z(hello_sem.at[0, r], hello_sem.at[1, r])
+
+        @pl.when(up)
+        def _():
+            pl.semaphore_wait(hello_sem.at[0, r], 1)
+
+        @pl.when(down)
+        def _():
+            pl.semaphore_wait(hello_sem.at[1, r], 1)
+
+    for i, device in enumerate((pair_dev, freq_dev)):
+        greet(pair_hello.at[i], device)
+        pl.semaphore_wait(pair_hello.at[i], 1)
+
+    acc[...] = jnp.zeros_like(acc)
+
+    @pl.loop(0, 2 * nq)
+    def _(q):
         own_copy(q).wait()
-
-        @pl.when(jnp.logical_and(inner, i < nq + kept))
-        def _():
-            back_copy(g_own.at[q], 0, i - nq).start()
-
-        @pl.when(jnp.logical_and(outer, i >= nq + kept))
-        def _():
-            up_copy(g_own.at[q], 0, i).start()
 
     @pl.loop(0, n)
     def _(j):
         w_own_copy(j).wait()
 
-    @pl.when(outer)
-    def _():
-        up_weights(w_own.at[last_block, :, my_rows, :], 0).start()
-
-    @pl.loop(0, 3)
-    def _(r):
-        along_z(hello_sem.at[0, r], hello_sem.at[1, r])
-
-        @pl.when(up)
-        def _():
-            pl.semaphore_wait(hello_sem.at[0, r], 1)
-
-        @pl.when(down)
-        def _():
-            pl.semaphore_wait(hello_sem.at[1, r], 1)
-
-    for i, device in enumerate((pair_dev, freq_dev)):
-        greet(pair_hello.at[i], device)
-        pl.semaphore_wait(pair_hello.at[i], 1)
-
-    acc[...] = jnp.zeros_like(acc)
+    def product(w, gi, gj, s):
+        lanes = slice(s * LANES, (s + 1) * LANES)
+        both = jnp.concatenate([gj[0, :, lanes], gj[1, :, lanes]], axis=1)
+        ab = jnp.dot(w[...].reshape(2 * h, h), both, preferred_element_type=jnp.float32)
+        a, b = ab[:h], ab[h:]
+        t = gi[0, :, lanes].astype(jnp.float32) * (a[:, :LANES] - b[:, LANES:])
+        t = t + gi[1, :, lanes].astype(jnp.float32) * (a[:, LANES:] + b[:, :LANES])
+        return jnp.sum(t.reshape(h // 8, 8, LANES), axis=0)
 
     def contribute(w, gi, gj, q, weight):
         for s in range(sub):
-            lanes = slice(s * LANES, (s + 1) * LANES)
-            both = jnp.concatenate([gj[0, :, lanes], gj[1, :, lanes]], axis=1)
-            ab = jnp.dot(w[...].reshape(2 * h, h), both, preferred_element_type=jnp.float32)
-            a, b = ab[:h], ab[h:]
-            t = gi[0, :, lanes].astype(jnp.float32) * (a[:, :LANES] - b[:, LANES:])
-            t = t + gi[1, :, lanes].astype(jnp.float32) * (a[:, LANES:] + b[:, :LANES])
-            t = jnp.sum(t.reshape(h // 8, 8, LANES), axis=0)
-            acc[q * sub + s] += t * weight
+            acc[q * sub + s] += product(w, gi, gj, s) * weight
 
     own_pair_block = block_of(z, 1)
 
@@ -707,6 +706,38 @@
         ref = part.at[source]
         return remote(ref, ref, part_send.at[k - 1], part_recv.at[k - 1], at_rank(flipped(k)))
 
+    my_group = (hi * 2 + parity) * n_freq + fq
+    late_rows = late * sub
+
+    def extra_copy(k):
+        def turned(v, bit):
+            return 1 - v if k & bit else v
+
+        target_z = 2 * turned(hi, 8) + turned(lax.rem(z, 2), 4)
+        target = {"stn": 2 * target_z + turned(parity, 2), "freq": turned(fq, 1)}
+        ref = extras.at[my_group]
+        return remote(ref, ref, extra_send.at[k - 1], extra_recv.at[my_group], target)
+
+    def finish():
+        first = (r_base + nq - late) * sub
+        q, slot = r_base + nq - 1, steps - 1
+        j = far_block(3)
+        for c in range(late_rows - sub):
+            row = jnp.sum(acc[first + c], axis=0, keepdims=True) / stations
+            extras[my_group, c] = row
+        wait_far(slot)
+        for s in range(sub):
+            gj = far.at[slot]
+            t = product(w_own.at[j], g_own.at[q], gj, s)
+            t = t + product(w_pair.at[j], g_pair.at[q], gj, s)
+            for p in range(2):
+                t = t + product(w_edge.at[p], near.at[p, q], gj, s)
+            t = acc[q * sub + s] + 2.0 * t
+            row = jnp.sum(t, axis=0, keepdims=True) / stations
+            extras[my_group, late_rows - sub + s] = row
+        for k in FAR_FIRST:
+            extra_copy(k).start()
+
     near_second = 2 * nq - kept + 1
     near_third = 3 * nq - kept + 2
     near_end = 4 * nq - 2 * kept + 2
@@ -722,7 +753,7 @@
 
     @pl.when(inner)
     def _():
-        @pl.loop(0, steps)
+        @pl.loop(0, steps - 1)
         def _(t):
             has_near, p, i = near_at(t)
             has_pair = jnp.logical_and(t >= nq, t < 3 * nq)
@@ -825,6 +856,8 @@
                 @pl.loop((nq - late) * sub, nq * sub)
                 def _(c):
                     acc[r_base * sub + c] = jnp.zeros((8, LANES), jnp.float32)
+
+        finish()
 
     @pl.when(outer)
     def _():
@@ -900,26 +933,6 @@
 
         share_part()
 
-    my_group = hi * 2 * n_freq + parity * n_freq + fq
-    late_rows = late * sub
-
-    def extra_copy(k, group):
-        ref = extras.at[group]
-        return remote(
-            extras.at[my_group], ref, extra_send.at[k - 1], extra_recv.at[group],
-            at_rank(flipped(k)),
-        )
-
-    @pl.when(inner)
-    def _():
-        for c in range(late_rows):
-            row = jnp.sum(acc[(r_base + nq - late) * sub + c], axis=0, keepdims=True) / stations
-            extras[my_group, c] = row
-
-        @pl.loop(0, total - 1)
-        def _(k):
-            extra_copy(total - 1 - k, my_group).start()
-
     @pl.loop(1, total // 2)
     def _(k):
         part_copy(k, flipped(k)).wait_recv()
@@ -935,6 +948,53 @@
         return remote(ref, ref, side_sem.at[0], side_sem.at[1], across_dev)
 
     side_copy(hi).start()
+
+    @pl.loop(0, 2 * nq)
+    def _(i):
+        pair_copy(i).wait_send()
+
+    @pl.loop(0, n)
+    def _(j):
+        w_pair_copy(j).wait_send()
+
+    sibling_copy(my_rows).wait_send()
+
+    @pl.loop(1, total // 2)
+    def _(k):
+        part_copy(k, rank).wait_send()
+
+    @pl.when(inner)
+    def _():
+        @pl.loop(0, steps)
+        def _(t):
+            mid_copy(far.at[t], t).wait_send()
+
+            @pl.when(t < 3 * nq + kept)
+            def _():
+                down_copy(t).wait_send()
+
+        @pl.loop(0, 2 * kept)
+        def _(i):
+            back_copy(g_own.at[0], i // kept, lax.rem(i, kept)).wait_send()
+
+        for k in FAR_FIRST:
+            extra_copy(k).wait_send()
+
+        edge_sibling_copy(my_rows).wait_send()
+
+    @pl.when(outer)
+    def _():
+        @pl.loop(0, 4 * nq)
+        def _(s):
+            i = lax.rem(s, 2 * nq)
+
+            @pl.when(jnp.logical_or(i < nq, i >= nq + kept))
+            def _():
+                up_copy(g_own.at[0], s // (2 * nq), i).wait_send()
+
+        for r in range(2):
+            up_weights(w_edge.at[r, :, my_rows, :], r).wait_send()
+
     side_copy(1 - hi).wait_recv()
     extra[...] = side[0] + side[1]
 
@@ -958,54 +1018,7 @@
     max_copy = remote(max_out, max_in, max_sem.at[0], max_sem.at[1], core_dev)
     max_copy.start()
 
-    @pl.loop(0, 2 * nq)
-    def _(i):
-        pair_copy(i).wait_send()
-
-    @pl.loop(0, n)
-    def _(j):
-        w_pair_copy(j).wait_send()
-
-    sibling_copy(my_rows).wait_send()
     side_copy(hi).wait_send()
-
-    @pl.loop(1, total // 2)
-    def _(k):
-        part_copy(k, rank).wait_send()
-
-    @pl.when(inner)
-    def _():
-        @pl.loop(0, steps)
-        def _(t):
-            mid_copy(far.at[t], t).wait_send()
-
-            @pl.when(t < 3 * nq + kept)
-            def _():
-                down_copy(t).wait_send()
-
-        @pl.loop(0, 2 * kept)
-        def _(i):
-            back_copy(g_own.at[0], i // kept, lax.rem(i, kept)).wait_send()
-
-        @pl.loop(1, total)
-        def _(k):
-            extra_copy(k, my_group).wait_send()
-
-        edge_sibling_copy(my_rows).wait_send()
-
-    @pl.when(outer)
-    def _():
-        @pl.loop(0, 4 * nq)
-        def _(s):
-            i = lax.rem(s, 2 * nq)
-
-            @pl.when(jnp.logical_or(i < nq, i >= nq + kept))
-            def _():
-                up_copy(g_own.at[0], s // (2 * nq), i).wait_send()
-
-        for r in range(2):
-            up_weights(w_edge.at[r, :, my_rows, :], r).wait_send()
-
     max_copy.wait()
     largest = jnp.maximum(max_out[0:1, 0:1], max_in[0:1, 0:1])
     out[...] = raw / (largest + 1e-6)
@@ -1024,7 +1037,7 @@
     total = n * n_freq
     out = pl.pallas_call(
         functools.partial(line_kernel, n_freq, h, stations, chunk, nq, kept, late, blocked),
-        out_shape=jax.ShapeDtypeStruct((rows, LANES), f32),
+        out_shape=pltpu.VMEM((rows, LANES), f32),
         in_specs=[pl.BlockSpec(memory_space=pl.ANY)] * 2,
         out_specs=pl.BlockSpec(memory_space=pltpu.VMEM),
         scratch_shapes=[

time: 107 us -> 105 us (0.981)
  Pallas kernels: 106 us -> 104 us
    pallas_call x1, Pallas kernels: 106 us -> 104 us  [line_body(): pl.pallas_call(functools.partial(line_kernel, n_freq, h, stations, chunk,...]
where the time goes in v2:
time: 105 us
  Pallas kernels  104 us (99%)
    pallas_call x1, Pallas kernels, line_body(): pl.pallas_call(functools.partial(line_kernel, n_freq, h, stations, chunk,...  104 us

profile of v2, /device:TPU:0, one launch (start us, length us, event | category | flops | bytes accessed | tf_op | source)
XLA Modules:
  0.0 104.7 jit_solution(1125838484613760554)
XLA Ops:
  0.0 104.0 %shard_map.28 = f32[16,128]{1,0:T(8,128)S(1)} custom-call(bf16[2,2,256,2048]{3,2,1,0:T(8,128)(2,1)} %greens.1, bf16[2,2,256,2048]{3,2,1,0:T(8,128)(2,1)} %weights.1), custom_call_target="tpu_custom_call" | custom-call | tf_op jit(solution)/shard_map/pallas_call | solution.py:1038
  104.1 0.6 copy.4

commit v3 on v2

--- a/solution.py
+++ b/solution.py
@@ -435,16 +435,16 @@
     return out.reshape(points)
 
 
-FAR_FIRST = (11, 9, 10, 8, 15, 7, 13, 14, 5, 6, 12, 4, 3, 1, 2)
+FAR_FIRST = (11, 9, 10, 8, 15, 7, 13, 14, 5, 6, 12, 4, 3, 1, 2, 0)
 
 
 def line_kernel(
     n_freq, h, stations, chunk, nq, kept, late, blocked,
     greens, weights, out,
-    g_own, g_pair, near, far, w_own, w_pair, w_edge, acc, part, side, extra, extras, max_out, max_in,
+    g_own, g_pair, near, far, w_own, w_pair, w_edge, acc, part, side, sums, extras,
     own_sem, w_own_sem, pair_send, pair_recv, wp_send, wp_recv, sib_sem, we_send, we_recv, we_sib,
     in_send, near_recv, far_recv, down_send, back_send, part_send, part_recv, side_sem,
-    extra_send, extra_recv, max_sem, hello_sem, pair_hello,
+    extra_send, extra_recv, base_sem, hello_sem, pair_hello,
 ):
     n = 8
     sub = chunk // LANES
@@ -468,7 +468,7 @@
     out_dev = {"stn": me - inward}
     core_dev = {"pts": 1 - core}
     freq_dev = {"freq": n_freq - 1 - fq}
-    across_dev = {"stn": lax.rem(me + n // 2, n)}
+    across_dev = {"stn": 2 * (3 - z) + parity}
     other_inner = 2 - hi
     other_edge = 3 - 3 * hi
     near_z = jnp.where(inner, z - inward // 2, z + inward // 2)
@@ -615,7 +615,7 @@
         def _():
             pl.semaphore_wait(hello_sem.at[1, r], 1)
 
-    for i, device in enumerate((pair_dev, freq_dev)):
+    for i, device in enumerate((pair_dev, freq_dev, core_dev)):
         greet(pair_hello.at[i], device)
         pl.semaphore_wait(pair_hello.at[i], 1)
 
@@ -709,14 +709,21 @@
     my_group = (hi * 2 + parity) * n_freq + fq
     late_rows = late * sub
 
-    def extra_copy(k):
+    sends = [(k, other) for k in FAR_FIRST for other in range(2) if k or other]
+
+    def extra_copy(k, other):
         def turned(v, bit):
             return 1 - v if k & bit else v
 
         target_z = 2 * turned(hi, 8) + turned(lax.rem(z, 2), 4)
-        target = {"stn": 2 * target_z + turned(parity, 2), "freq": turned(fq, 1)}
-        ref = extras.at[my_group]
-        return remote(ref, ref, extra_send.at[k - 1], extra_recv.at[my_group], target)
+        target = {
+            "stn": 2 * target_z + turned(parity, 2), "freq": turned(fq, 1),
+            "pts": 1 - core if other else core,
+        }
+        return remote(
+            extras.at[0, my_group], extras.at[other, my_group],
+            extra_send.at[other, k], extra_recv.at[other], target,
+        )
 
     def finish():
         first = (r_base + nq - late) * sub
@@ -724,7 +731,7 @@
         j = far_block(3)
         for c in range(late_rows - sub):
             row = jnp.sum(acc[first + c], axis=0, keepdims=True) / stations
-            extras[my_group, c] = row
+            extras[0, my_group, c] = row
         wait_far(slot)
         for s in range(sub):
             gj = far.at[slot]
@@ -734,9 +741,9 @@
                 t = t + product(w_edge.at[p], near.at[p, q], gj, s)
             t = acc[q * sub + s] + 2.0 * t
             row = jnp.sum(t, axis=0, keepdims=True) / stations
-            extras[my_group, late_rows - sub + s] = row
-        for k in FAR_FIRST:
-            extra_copy(k).start()
+            extras[0, my_group, late_rows - sub + s] = row
+        for k, other in sends:
+            extra_copy(k, other).start()
 
     near_second = 2 * nq - kept + 1
     near_third = 3 * nq - kept + 2
@@ -948,6 +955,10 @@
         return remote(ref, ref, side_sem.at[0], side_sem.at[1], across_dev)
 
     side_copy(hi).start()
+    side_copy(1 - hi).wait_recv()
+    sums[0] = side[0] + side[1]
+    base_copy = remote(sums.at[0], sums.at[1], base_sem.at[0], base_sem.at[1], core_dev)
+    base_copy.start()
 
     @pl.loop(0, 2 * nq)
     def _(i):
@@ -977,8 +988,8 @@
         def _(i):
             back_copy(g_own.at[0], i // kept, lax.rem(i, kept)).wait_send()
 
-        for k in FAR_FIRST:
-            extra_copy(k).wait_send()
+        for k, other in sends:
+            extra_copy(k, other).wait_send()
 
         edge_sibling_copy(my_rows).wait_send()
 
@@ -995,32 +1006,34 @@
         for r in range(2):
             up_weights(w_edge.at[r, :, my_rows, :], r).wait_send()
 
-    side_copy(1 - hi).wait_recv()
-    extra[...] = side[0] + side[1]
-
-    @pl.loop(0, 4 * n_freq)
-    def _(g):
-        @pl.when(jnp.logical_or(outer, g != my_group))
-        def _():
-            ref = extras.at[g]
-            remote(ref, ref, extra_send.at[0], extra_recv.at[g], pair_dev).wait_recv()
-
-    for low in range(2):
-        for c in range(late_rows):
-            row = extras[low * 2 * n_freq, c]
-            for g in range(1, 2 * n_freq):
-                row = row + extras[low * 2 * n_freq + g, c]
-            at = ((1 - low) * nq + nq - late) * sub + c
-            extra[at:at + 1, :] += row
-
-    raw = extra[...]
-    max_out[...] = jnp.broadcast_to(jnp.max(jnp.abs(raw)), max_out.shape)
-    max_copy = remote(max_out, max_in, max_sem.at[0], max_sem.at[1], core_dev)
-    max_copy.start()
-
     side_copy(hi).wait_send()
-    max_copy.wait()
-    largest = jnp.maximum(max_out[0:1, 0:1], max_in[0:1, 0:1])
+
+    def wait_extras(which, groups):
+        ref = extras.at[which, pl.ds(0, groups)]
+        remote(ref, ref, extra_send.at[0, 0], extra_recv.at[which], core_dev).wait_recv()
+
+    @pl.when(inner)
+    def _():
+        wait_extras(0, 4 * n_freq - 1)
+
+    @pl.when(outer)
+    def _():
+        wait_extras(0, 4 * n_freq)
+
+    wait_extras(1, 4 * n_freq)
+    base_copy.wait()
+
+    for which in range(2):
+        for low in range(2):
+            for c in range(late_rows):
+                row = extras[which, low * 2 * n_freq, c]
+                for g in range(1, 2 * n_freq):
+                    row = row + extras[which, low * 2 * n_freq + g, c]
+                at = ((1 - low) * nq + nq - late) * sub + c
+                sums[which, at:at + 1, :] += row
+
+    raw = sums[0]
+    largest = jnp.max(jnp.maximum(jnp.abs(raw), jnp.abs(sums[1])), keepdims=True)
     out[...] = raw / (largest + 1e-6)
 
 
@@ -1051,16 +1064,14 @@
             pltpu.VMEM((rows, 8, LANES), f32),
             pltpu.VMEM((total, rows, LANES), f32),
             pltpu.VMEM((2, rows, LANES), f32),
-            pltpu.VMEM((rows, LANES), f32),
-            pltpu.VMEM((4 * n_freq, late_rows, 1, LANES), f32),
-            pltpu.VMEM((8, LANES), f32),
-            pltpu.VMEM((8, LANES), f32),
+            pltpu.VMEM((2, rows, LANES), f32),
+            pltpu.VMEM((2, 4 * n_freq, late_rows, 1, LANES), f32),
             dma((2 * nq,)), dma((n,)), dma((2 * nq,)), dma((2 * nq,)), dma((n,)), dma((n,)), dma((2,)),
             dma((2,)), dma((2,)), dma((2,)),
             dma((4 * nq,)), dma((4 * nq,)), dma((4 * nq,)), dma((4 * nq,)), dma((2 * kept,)),
             dma((total // 2 - 1,)), dma((total // 2 - 1,)), dma((2,)),
-            dma((total - 1,)), dma((4 * n_freq,)), dma((2,)),
-            regular((2, 3)), regular((2,)),
+            dma((2, total)), dma((2,)), dma((2,)),
+            regular((2, 3)), regular((3,)),
         ],
         compiler_params=pltpu.CompilerParams(
             collective_id=0, has_side_effects=True, vmem_limit_bytes=60 * 1024 * 1024

time: 105 us -> 104 us (level)
  no operation moved by 1% of the time
where the time goes in v3:
time: 104 us
  Pallas kernels  103 us (99%)
    pallas_call x1, Pallas kernels, line_body(): pl.pallas_call(functools.partial(line_kernel, n_freq, h, stations, chunk,...  103 us

profile of v3, /device:TPU:0, one launch (start us, length us, event | category | flops | bytes accessed | tf_op | source)
XLA Modules:
  0.0 103.8 jit_solution(11929746532879939002)
XLA Ops:
  0.0 103.2 %shard_map.28 = f32[16,128]{1,0:T(8,128)S(1)} custom-call(bf16[2,2,256,2048]{3,2,1,0:T(8,128)(2,1)} %greens.1, bf16[2,2,256,2048]{3,2,1,0:T(8,128)(2,1)} %weights.1), custom_call_target="tpu_custom_call" | custom-call | tf_op jit(solution)/shard_map/pallas_call | solution.py:1051
  103.2 0.6 copy.4

commit v4 on v3

--- a/solution.py
+++ b/solution.py
@@ -441,10 +441,10 @@
 def line_kernel(
     n_freq, h, stations, chunk, nq, kept, late, blocked,
     greens, weights, out,
-    g_own, g_pair, near, far, w_own, w_pair, w_edge, acc, part, side, sums, extras,
+    g_own, g_pair, near, far, w_own, w_pair, w_edge, folded, acc, part, side, sums, extras,
     own_sem, w_own_sem, pair_send, pair_recv, wp_send, wp_recv, sib_sem, we_send, we_recv, we_sib,
     in_send, near_recv, far_recv, down_send, back_send, part_send, part_recv, side_sem,
-    extra_send, extra_recv, base_sem, hello_sem, pair_hello,
+    extra_send, extra_recv, base_sem, fold_sem, hello_sem, pair_hello,
 ):
     n = 8
     sub = chunk // LANES
@@ -487,7 +487,6 @@
     def far_block(e):
         return block_of(jnp.where(lax.rem(e, 2) == 0, other_inner, other_edge), e // 2)
 
-    last_block = block_of(other_edge, 1)
     every_row = pl.ds(0, h)
     my_rows = pl.ds(pl.multiple_of(core * half_rows, 8), half_rows)
     sib_rows = pl.ds(pl.multiple_of((1 - core) * half_rows, 8), half_rows)
@@ -522,18 +521,22 @@
         return remote(part_of_w, part_of_w, sib_sem.at[0], sib_sem.at[1], core_dev)
 
     def edge_sibling_copy(rows):
-        part_of_w = w_edge.at[:, :, rows, :]
+        part_of_w = w_edge.at[:, :, :, rows, :]
         return remote(part_of_w, part_of_w, we_sib.at[0], we_sib.at[1], core_dev)
 
     def up_copy(src, p, i):
         slot = p * 2 * nq + i
         return remote(src, near.at[p, pair_q(i)], in_send.at[slot], near_recv.at[slot], in_dev)
 
-    def up_weights(src, p):
-        return remote(src, w_edge.at[p, :, my_rows, :], we_send.at[p], we_recv.at[p], in_dev)
+    def up_weights(src, b, p):
+        i = 2 * b + p
+        return remote(src, w_edge.at[b, p, :, my_rows, :], we_send.at[i], we_recv.at[i], in_dev)
 
     def mid_copy(src, slot):
-        return remote(src, far.at[slot], in_send.at[slot], far_recv.at[slot], in_dev)
+        last = slot == steps - 1
+        land = jnp.where(jnp.logical_and(last, core == 0), steps, slot)
+        target = {"stn": me + inward, "pts": jnp.where(last, 1, core)}
+        return remote(src, far.at[land], in_send.at[slot], far_recv.at[land], target)
 
     def down_copy(slot):
         return remote(far.at[slot], far.at[slot], down_send.at[slot], far_recv.at[slot], out_dev)
@@ -601,7 +604,8 @@
 
     @pl.when(outer)
     def _():
-        up_weights(w_src(parity, last_block, my_rows), 0).start()
+        for b in range(2):
+            up_weights(w_src(parity, far_block(2 + b), my_rows), b, 0).start()
 
     @pl.loop(0, 3)
     def _(r):
@@ -660,16 +664,53 @@
     def near_work(p, q, w, g):
         contribute(w.at[block_of(near_z, p)], g.at[q], near.at[p, q], q, 2.0)
 
-    def edge_work(c):
+    def edge_work(b, c):
         q = r_base + c
 
         @pl.loop(0, 2)
         def _(p):
-            contribute(w_edge.at[p], near.at[p, q], far.at[3 * nq + c], q, 2.0)
+            contribute(w_edge.at[b, p], near.at[p, q], far.at[(2 + b) * nq + c], q, 2.0)
+
+    def transposed(w, g):
+        return lax.dot_general(w, g, (((0,), (0,)), ((), ())), preferred_element_type=jnp.float32)
+
+    def fold(w, gi, s):
+        lanes = slice(s * LANES, (s + 1) * LANES)
+        both = jnp.concatenate([gi[0, :, lanes], gi[1, :, lanes]], axis=1)
+        a, b = transposed(w[0], both), transposed(w[1], both)
+        return a[:, :LANES] + b[:, LANES:], a[:, LANES:] - b[:, :LANES]
+
+    def fold_last():
+        q, j = r_base + nq - 1, far_block(3)
+        for s in range(sub):
+            lanes = slice(s * LANES, (s + 1) * LANES)
+            re, im = fold(w_own.at[j], g_own.at[q], s)
+            folded[core, 0, :, lanes] = re
+            folded[core, 1, :, lanes] = im
+            for w, g in ((w_pair.at[j], g_pair.at[q]), (w_edge.at[1, 0], near.at[0, q]), (w_edge.at[1, 1], near.at[1, q])):
+                re, im = fold(w, g, s)
+                folded[core, 0, :, lanes] += re
+                folded[core, 1, :, lanes] += im
+
+        @pl.when(core == 0)
+        def _():
+            fold_copy().start()
+
+    def fold_copy():
+        return remote(folded.at[0], folded.at[0], fold_sem.at[0], fold_sem.at[1], core_dev)
+
+    def unfold(which, slot, s):
+        lanes = slice(s * LANES, (s + 1) * LANES)
+        t = far[slot, 0, :, lanes].astype(jnp.float32) * folded[which, 0, :, lanes]
+        t = t + far[slot, 1, :, lanes].astype(jnp.float32) * folded[which, 1, :, lanes]
+        return 2.0 * jnp.sum(t.reshape(h // 8, 8, LANES), axis=0)
+
+    def passed_down(t):
+        return jnp.logical_or(t < 2 * nq, lax.rem(t, nq) < kept)
 
     def wait_far(t):
         ref = far.at[t]
-        remote(ref, ref, down_send.at[t], far_recv.at[t], in_dev).wait_recv()
+        remote(ref, ref, in_send.at[0], far_recv.at[t], in_dev).wait_recv()
 
     def wait_near(p, i):
         slot = p * 2 * nq + i
@@ -721,42 +762,44 @@
             "pts": 1 - core if other else core,
         }
         return remote(
-            extras.at[0, my_group], extras.at[other, my_group],
-            extra_send.at[other, k], extra_recv.at[other], target,
+            extras.at[core, my_group], extras.at[core, my_group],
+            extra_send.at[other, k], extra_recv.at[core], target,
         )
+
+    def late_row(t):
+        return jnp.sum(t, axis=0, keepdims=True) / stations
 
     def finish():
         first = (r_base + nq - late) * sub
-        q, slot = r_base + nq - 1, steps - 1
-        j = far_block(3)
-        for c in range(late_rows - sub):
-            row = jnp.sum(acc[first + c], axis=0, keepdims=True) / stations
-            extras[0, my_group, c] = row
-        wait_far(slot)
+        for c in range(late_rows):
+            extras[core, my_group, c] = late_row(acc[first + c])
         for s in range(sub):
-            gj = far.at[slot]
-            t = product(w_own.at[j], g_own.at[q], gj, s)
-            t = t + product(w_pair.at[j], g_pair.at[q], gj, s)
-            for p in range(2):
-                t = t + product(w_edge.at[p], near.at[p, q], gj, s)
-            t = acc[q * sub + s] + 2.0 * t
-            row = jnp.sum(t, axis=0, keepdims=True) / stations
-            extras[0, my_group, late_rows - sub + s] = row
+            extras[core, my_group, late_rows + s] = jnp.zeros((1, LANES), jnp.float32)
+
+        @pl.when(core == 1)
+        def _():
+            fold_copy().wait_recv()
+            wait_far(steps)
+            wait_far(steps - 1)
+            for s in range(sub):
+                c = late_rows - sub + s
+                extras[1, my_group, c] = late_row(acc[first + c] + unfold(1, steps - 1, s))
+                extras[1, my_group, late_rows + s] = late_row(unfold(0, steps, s))
+
         for k, other in sends:
             extra_copy(k, other).start()
 
-    near_second = 2 * nq - kept + 1
-    near_third = 3 * nq - kept + 2
-    near_end = 4 * nq - 2 * kept + 2
+    near_second = 2 * nq - kept + 4
+    near_third = near_second + nq
+    near_end = near_third + nq - kept
 
     def near_at(t):
         second = t >= near_second
-        third = t >= near_third
         i = jnp.where(t < nq, t, t + kept)
         i = jnp.where(second, t - near_second, i)
-        i = jnp.where(third, t - near_third + nq + kept, i)
-        present = jnp.logical_and(t != near_second - 1, t != near_third - 1)
-        return jnp.logical_and(present, t < near_end), second.astype(jnp.int32), i
+        i = jnp.where(t >= near_third, t - near_third + nq + kept, i)
+        present = jnp.logical_or(t < 2 * nq - kept, jnp.logical_and(second, t < near_end))
+        return present, second.astype(jnp.int32), i
 
     @pl.when(inner)
     def _():
@@ -767,7 +810,7 @@
             turn = t - nq
             wait_far(t)
 
-            @pl.when(t < 3 * nq + kept)
+            @pl.when(passed_down(t))
             def _():
                 down_copy(t).start()
 
@@ -799,13 +842,14 @@
             def _():
                 sibling_copy(sib_rows).wait_recv()
 
-            @pl.when(t == 3 * nq + kept - 1)
-            def _():
-                for r in range(2):
-                    up_weights(w_edge.at[r, :, my_rows, :], r).wait_recv()
+            @pl.when(t == near_second)
+            def _():
+                for r in range(4):
+                    part_of_w = w_edge.at[r // 2, r % 2, :, my_rows, :]
+                    up_weights(part_of_w, r // 2, r % 2).wait_recv()
                 edge_sibling_copy(my_rows).start()
 
-            @pl.when(t == 3 * nq + kept)
+            @pl.when(t == near_second + 2)
             def _():
                 edge_sibling_copy(sib_rows).wait_recv()
 
@@ -824,6 +868,10 @@
                 def _():
                     near_work(p, q, w_pair, g_pair)
 
+                    @pl.when(i >= nq)
+                    def _():
+                        edge_work(0, i - nq)
+
             @pl.when(has_pair)
             def _():
                 cross_work(pair_q(turn))
@@ -854,7 +902,7 @@
 
             @pl.when(t >= 3 * nq + kept)
             def _():
-                edge_work(t - 3 * nq)
+                edge_work(1, t - 3 * nq)
 
             @pl.when(t == steps - late - 1)
             def _():
@@ -864,19 +912,28 @@
                 def _(c):
                     acc[r_base * sub + c] = jnp.zeros((8, LANES), jnp.float32)
 
+            @pl.when(t == near_end - 1)
+            def _():
+                fold_last()
+
         finish()
 
     @pl.when(outer)
     def _():
-        @pl.loop(0, 3 * nq + kept)
+        @pl.loop(0, 3 * nq)
         def _(t):
             turn = t - nq + 2
             has_pair = jnp.logical_and(turn >= 0, turn < 2 * nq)
             back = t - 2 * nq - 4
+            has_back = jnp.logical_and(back >= 0, back < kept)
+            slot = jnp.where(t < 2 * nq + kept, t, t + nq - kept)
+            has_far = t < 2 * nq + 2 * kept
 
             @pl.when(turn == 0)
             def _():
                 wait_w_pair()
+                for b in range(2):
+                    up_weights(w_pair.at[far_block(2 + b), :, my_rows, :], b, 1).start()
 
             @pl.when(has_pair)
             def _():
@@ -886,10 +943,6 @@
                 def _():
                     up_copy(g_pair.at[pair_q(turn)], 1, turn).start()
 
-                @pl.when(turn == nq - 1)
-                def _():
-                    up_weights(w_pair.at[last_block, :, my_rows, :], 1).start()
-
             @pl.when(t == nq)
             def _():
                 sibling_copy(sib_rows).wait_recv()
@@ -898,12 +951,18 @@
             def _():
                 wait_near(0, nq + t)
 
-            @pl.when(jnp.logical_and(back >= 0, back < kept))
+            @pl.when(has_back)
             def _():
                 wait_near(1, nq + back)
 
-            wait_far(t)
-            far_work(t, w_own, g_own)
+            @pl.when(has_far)
+            def _():
+                wait_far(slot)
+                far_work(slot, w_own, g_own)
+
+            @pl.when(jnp.logical_and(has_far, t >= 2 * nq))
+            def _():
+                far_work(slot, w_pair, g_pair)
 
             @pl.when(t < 2 * nq)
             def _():
@@ -913,7 +972,7 @@
             def _():
                 near_work(0, r_base + t, w_own, g_own)
 
-            @pl.when(jnp.logical_and(back >= 0, back < kept))
+            @pl.when(has_back)
             def _():
                 q = r_base + back
                 near_work(0, q, w_pair, g_pair)
@@ -924,19 +983,15 @@
             def _():
                 cross_work(pair_q(turn))
 
-            @pl.when(jnp.logical_and(t >= nq, t < 3 * nq))
+            @pl.when(t >= nq)
             def _():
                 pair_work(pair_q(t - nq))
 
-            @pl.when(jnp.logical_and(t >= 2 * nq, t < 3 * nq))
-            def _():
-                @pl.loop(0, 3)
+            @pl.when(t >= 2 * nq)
+            def _():
+                @pl.loop(0, 2)
                 def _(e):
                     far_work(e * nq + t - 2 * nq, w_pair, g_pair)
-
-            @pl.when(t >= 3 * nq)
-            def _():
-                far_work(t, w_pair, g_pair)
 
         share_part()
 
@@ -956,8 +1011,8 @@
 
     side_copy(hi).start()
     side_copy(1 - hi).wait_recv()
-    sums[0] = side[0] + side[1]
-    base_copy = remote(sums.at[0], sums.at[1], base_sem.at[0], base_sem.at[1], core_dev)
+    sums[core] = side[0] + side[1]
+    base_copy = remote(sums.at[core], sums.at[core], base_sem.at[0], base_sem.at[1], core_dev)
     base_copy.start()
 
     @pl.loop(0, 2 * nq)
@@ -978,9 +1033,9 @@
     def _():
         @pl.loop(0, steps)
         def _(t):
-            mid_copy(far.at[t], t).wait_send()
-
-            @pl.when(t < 3 * nq + kept)
+            mid_copy(far.at[0], t).wait_send()
+
+            @pl.when(passed_down(t))
             def _():
                 down_copy(t).wait_send()
 
@@ -992,6 +1047,10 @@
             extra_copy(k, other).wait_send()
 
         edge_sibling_copy(my_rows).wait_send()
+
+        @pl.when(core == 0)
+        def _():
+            fold_copy().wait_send()
 
     @pl.when(outer)
     def _():
@@ -1003,8 +1062,9 @@
             def _():
                 up_copy(g_own.at[0], s // (2 * nq), i).wait_send()
 
-        for r in range(2):
-            up_weights(w_edge.at[r, :, my_rows, :], r).wait_send()
+        for r in range(4):
+            part_of_w = w_edge.at[r // 2, r % 2, :, my_rows, :]
+            up_weights(part_of_w, r // 2, r % 2).wait_send()
 
     side_copy(hi).wait_send()
 
@@ -1014,33 +1074,41 @@
 
     @pl.when(inner)
     def _():
-        wait_extras(0, 4 * n_freq - 1)
+        wait_extras(core, 4 * n_freq - 1)
+        wait_extras(1 - core, 4 * n_freq)
 
     @pl.when(outer)
     def _():
         wait_extras(0, 4 * n_freq)
-
-    wait_extras(1, 4 * n_freq)
-    base_copy.wait()
+        wait_extras(1, 4 * n_freq)
+
+    base_copy.wait_send()
+    sum_ref = sums.at[1 - core]
+    remote(sum_ref, sum_ref, base_sem.at[0], base_sem.at[1], core_dev).wait_recv()
+
+    def late_sum(which, low, c):
+        row = extras[which, low * 2 * n_freq, c]
+        for g in range(1, 2 * n_freq):
+            row = row + extras[which, low * 2 * n_freq + g, c]
+        return row
 
     for which in range(2):
         for low in range(2):
             for c in range(late_rows):
-                row = extras[which, low * 2 * n_freq, c]
-                for g in range(1, 2 * n_freq):
-                    row = row + extras[which, low * 2 * n_freq + g, c]
+                row = late_sum(which, low, c)
+                if which == 0 and c >= late_rows - sub:
+                    row = row + late_sum(1, low, c + sub)
                 at = ((1 - low) * nq + nq - late) * sub + c
                 sums[which, at:at + 1, :] += row
 
-    raw = sums[0]
-    largest = jnp.max(jnp.maximum(jnp.abs(raw), jnp.abs(sums[1])), keepdims=True)
-    out[...] = raw / (largest + 1e-6)
+    largest = jnp.max(jnp.maximum(jnp.abs(sums[0]), jnp.abs(sums[1])), keepdims=True)
+    out[...] = sums[core] / (largest + 1e-6)
 
 
 def line_body(n_freq, chunk, nq, blocked, greens, weights):
     _, _, h, points = greens.shape
     n = 8
-    kept, late = nq // 4, 3
+    kept, late = 3 * nq // 8, 3
     stations = n * h
     dma = pltpu.SemaphoreType.DMA
     regular = pltpu.SemaphoreType.REGULAR
@@ -1057,20 +1125,21 @@
             pltpu.VMEM((2 * nq, 2, h, chunk), bf16),
             pltpu.VMEM((2 * nq, 2, h, chunk), bf16),
             pltpu.VMEM((2, 2 * nq, 2, h, chunk), bf16),
-            pltpu.VMEM((4 * nq, 2, h, chunk), bf16),
+            pltpu.VMEM((4 * nq + 1, 2, h, chunk), bf16),
             pltpu.VMEM((n, 2, h, h), bf16),
             pltpu.VMEM((n, 2, h, h), bf16),
-            pltpu.VMEM((2, 2, h, h), bf16),
+            pltpu.VMEM((2, 2, 2, h, h), bf16),
+            pltpu.VMEM((2, 2, h, chunk), f32),
             pltpu.VMEM((rows, 8, LANES), f32),
             pltpu.VMEM((total, rows, LANES), f32),
             pltpu.VMEM((2, rows, LANES), f32),
             pltpu.VMEM((2, rows, LANES), f32),
-            pltpu.VMEM((2, 4 * n_freq, late_rows, 1, LANES), f32),
+            pltpu.VMEM((2, 4 * n_freq, late_rows + chunk // LANES, 1, LANES), f32),
             dma((2 * nq,)), dma((n,)), dma((2 * nq,)), dma((2 * nq,)), dma((n,)), dma((n,)), dma((2,)),
-            dma((2,)), dma((2,)), dma((2,)),
-            dma((4 * nq,)), dma((4 * nq,)), dma((4 * nq,)), dma((4 * nq,)), dma((2 * kept,)),
+            dma((4,)), dma((4,)), dma((2,)),
+            dma((4 * nq,)), dma((4 * nq,)), dma((4 * nq + 1,)), dma((4 * nq,)), dma((2 * kept,)),
             dma((total // 2 - 1,)), dma((total // 2 - 1,)), dma((2,)),
-            dma((2, total)), dma((2,)), dma((2,)),
+            dma((2, total)), dma((2,)), dma((2,)), dma((2,)),
             regular((2, 3)), regular((3,)),
         ],
         compiler_params=pltpu.CompilerParams(

time: 104 us -> 103 us (level)
  no operation moved by 1% of the time
where the time goes in v4:
time: 103 us
  Pallas kernels  102 us (99%)
    pallas_call x1, Pallas kernels, line_body(): pl.pallas_call(functools.partial(line_kernel, n_freq, h, stations, chunk,...  102 us

profile of v4, /device:TPU:0, one launch (start us, length us, event | category | flops | bytes accessed | tf_op | source)
XLA Modules:
  0.0 103.0 jit_solution(17135087117252631275)
XLA Ops:
  0.0 102.4 %shard_map.28 = f32[16,128]{1,0:T(8,128)S(1)} custom-call(bf16[2,2,256,2048]{3,2,1,0:T(8,128)(2,1)} %greens.1, bf16[2,2,256,2048]{3,2,1,0:T(8,128)(2,1)} %weights.1), custom_call_target="tpu_custom_call" | custom-call | tf_op jit(solution)/shard_map/pallas_call | solution.py:1119
  102.4 0.6 copy.4

commit v5 on v4

--- a/solution.py
+++ b/solution.py
@@ -444,7 +444,7 @@
     g_own, g_pair, near, far, w_own, w_pair, w_edge, folded, acc, part, side, sums, extras,
     own_sem, w_own_sem, pair_send, pair_recv, wp_send, wp_recv, sib_sem, we_send, we_recv, we_sib,
     in_send, near_recv, far_recv, down_send, back_send, part_send, part_recv, side_sem,
-    extra_send, extra_recv, base_sem, fold_sem, hello_sem, pair_hello,
+    extra_send, extra_recv, base_sem, fold_sem, reply_sem, hello_sem, pair_hello,
 ):
     n = 8
     sub = chunk // LANES
@@ -487,6 +487,27 @@
     def far_block(e):
         return block_of(jnp.where(lax.rem(e, 2) == 0, other_inner, other_edge), e // 2)
 
+    def position(e, c):
+        late_c = c >= jnp.where(e < 2, nq - 1, kept)
+        pair_half = jnp.where(e == 2, 2 * nq, 2 * nq + kept) + c
+        pair_late = jnp.where(e == 2, 2 * nq + kept, 3 * nq) + c
+        early = jnp.where(late_c, 2 * nq - 2 + e, e * (nq - 1) + c)
+        return jnp.where(e < 2, early, jnp.where(late_c, pair_late, pair_half))
+
+    def block_at(t):
+        e = (t >= nq - 1).astype(jnp.int32)
+        c = t - e * (nq - 1)
+        corner = t >= 2 * nq - 2
+        e = jnp.where(corner, t - (2 * nq - 2), e)
+        c = jnp.where(corner, nq - 1, c)
+        pairs = t - 2 * nq
+        third = jnp.logical_and(pairs >= kept, pairs < 2 * kept)
+        third = jnp.logical_or(third, pairs >= nq + kept)
+        pair_c = jnp.where(pairs < kept, pairs, jnp.where(pairs < nq + kept, pairs - kept, pairs - nq))
+        e = jnp.where(pairs >= 0, 2 + third.astype(jnp.int32), e)
+        c = jnp.where(pairs >= 0, pair_c, c)
+        return e, c
+
     every_row = pl.ds(0, h)
     my_rows = pl.ds(pl.multiple_of(core * half_rows, 8), half_rows)
     sib_rows = pl.ds(pl.multiple_of((1 - core) * half_rows, 8), half_rows)
@@ -538,6 +559,8 @@
         target = {"stn": me + inward, "pts": jnp.where(last, 1, core)}
         return remote(src, far.at[land], in_send.at[slot], far_recv.at[land], target)
 
+    corner = 2 * nq - 2
+
     def down_copy(slot):
         return remote(far.at[slot], far.at[slot], down_send.at[slot], far_recv.at[slot], out_dev)
 
@@ -563,22 +586,32 @@
         def _():
             greet(sem_down, {"stn": me - 2})
 
-    along_z(barrier, barrier)
+    @pl.when(inner)
+    def _():
+        greet(barrier, in_dev)
+        greet(barrier, out_dev)
+
     for device in greeted:
         greet(barrier, device)
-    pl.semaphore_wait(barrier, len(greeted) + up.astype(jnp.int32) + down.astype(jnp.int32))
+    pl.semaphore_wait(barrier, len(greeted) + 1)
+
+    @pl.when(outer)
+    def _():
+        greet(reply_sem.at[0], in_dev)
 
     @pl.loop(0, nq)
     def _(i):
         src = g_src(pair_q(i))
 
-        @pl.when(inner)
+        @pl.when(jnp.logical_and(inner, i < nq - 1))
         def _():
             mid_copy(src, i).start()
 
         @pl.when(outer)
         def _():
             up_copy(src, 0, i).start()
+
+    corner_src = g_src(pair_q(nq - 1))
 
     @pl.loop(0, n)
     def _(j):
@@ -590,17 +623,13 @@
         own_copy(pair_q(i)).start()
         pair_copy(i).start()
 
-    @pl.loop(nq, 2 * nq)
-    def _(i):
-        src = g_src(pair_q(i))
-
-        @pl.when(jnp.logical_and(inner, i < nq + kept))
-        def _():
-            back_copy(src, 0, i - nq).start()
-
-        @pl.when(jnp.logical_and(outer, i >= nq + kept))
-        def _():
-            up_copy(src, 0, i).start()
+    @pl.when(inner)
+    def _():
+        pl.semaphore_wait(reply_sem.at[0], 1)
+
+        @pl.loop(0, kept)
+        def _(c):
+            back_copy(g_src(pair_q(nq + c)), 0, c).start()
 
     @pl.when(outer)
     def _():
@@ -657,9 +686,9 @@
     def pair_work(q):
         contribute(w_pair.at[own_pair_block], g_pair.at[q], g_pair.at[q], q, 1.0)
 
-    def far_work(slot, w, g):
-        q = r_base + lax.rem(slot, nq)
-        contribute(w.at[far_block(slot // nq)], g.at[q], far.at[slot], q, 2.0)
+    def far_work(e, c, w, g):
+        q = r_base + c
+        contribute(w.at[far_block(e)], g.at[q], far.at[position(e, c)], q, 2.0)
 
     def near_work(p, q, w, g):
         contribute(w.at[block_of(near_z, p)], g.at[q], near.at[p, q], q, 2.0)
@@ -669,7 +698,7 @@
 
         @pl.loop(0, 2)
         def _(p):
-            contribute(w_edge.at[b, p], near.at[p, q], far.at[(2 + b) * nq + c], q, 2.0)
+            contribute(w_edge.at[b, p], near.at[p, q], far.at[position(2 + b, c)], q, 2.0)
 
     def transposed(w, g):
         return lax.dot_general(w, g, (((0,), (0,)), ((), ())), preferred_element_type=jnp.float32)
@@ -706,7 +735,7 @@
         return 2.0 * jnp.sum(t.reshape(h // 8, 8, LANES), axis=0)
 
     def passed_down(t):
-        return jnp.logical_or(t < 2 * nq, lax.rem(t, nq) < kept)
+        return t < 2 * nq + 2 * kept
 
     def wait_far(t):
         ref = far.at[t]
@@ -789,17 +818,19 @@
         for k, other in sends:
             extra_copy(k, other).start()
 
-    near_second = 2 * nq - kept + 4
+    near_second = nq + 4
     near_third = near_second + nq
-    near_end = near_third + nq - kept
+    near_fourth = near_third + nq - kept
+    near_end = near_fourth + nq - kept
 
     def near_at(t):
-        second = t >= near_second
-        i = jnp.where(t < nq, t, t + kept)
-        i = jnp.where(second, t - near_second, i)
+        i = jnp.where(t >= near_second, t - near_second, t)
         i = jnp.where(t >= near_third, t - near_third + nq + kept, i)
-        present = jnp.logical_or(t < 2 * nq - kept, jnp.logical_and(second, t < near_end))
-        return present, second.astype(jnp.int32), i
+        i = jnp.where(t >= near_fourth, t - near_fourth + nq + kept, i)
+        second = jnp.logical_and(t >= near_second, t < near_third)
+        p = jnp.logical_or(second, t >= near_fourth).astype(jnp.int32)
+        present = jnp.logical_or(t < nq, jnp.logical_and(t >= near_second, t < near_end))
+        return present, p, i
 
     @pl.when(inner)
     def _():
@@ -818,9 +849,13 @@
             def _():
                 wait_near(p, i)
 
-                @pl.when(i < nq)
-                def _():
-                    mid_copy(near.at[p, pair_q(i)], (2 * p + 1) * nq + i).start()
+            @pl.when(t < nq)
+            def _():
+                mid_copy(near.at[0, pair_q(t)], position(1, t)).start()
+
+            @pl.when(t == nq - 2)
+            def _():
+                mid_copy(corner_src, corner).start()
 
             @pl.when(t == nq)
             def _():
@@ -830,13 +865,30 @@
             def _():
                 pair_copy(turn).wait_recv()
 
-                @pl.when(turn < nq)
+                @pl.when(turn < kept)
                 def _():
                     mid_copy(g_pair.at[pair_q(turn)], 2 * nq + turn).start()
 
                 @pl.when(jnp.logical_and(turn >= nq, turn < nq + kept))
                 def _():
                     back_copy(g_pair.at[pair_q(turn)], 1, turn - nq).start()
+
+            third = t - near_second
+            fourth = third - (nq - kept)
+
+            @pl.when(jnp.logical_and(third >= 0, third < kept))
+            def _():
+                mid_copy(near.at[1, pair_q(third)], 2 * nq + kept + third).start()
+
+            send_third = jnp.logical_and(third >= kept, third < nq)
+
+            @pl.when(send_third)
+            def _():
+                mid_copy(g_pair.at[pair_q(third)], 2 * nq + kept + third).start()
+
+            @pl.when(jnp.logical_and(fourth >= kept, fourth < nq))
+            def _():
+                mid_copy(near.at[1, pair_q(fourth)], 3 * nq + fourth).start()
 
             @pl.when(t == nq + 2)
             def _():
@@ -853,7 +905,8 @@
             def _():
                 edge_sibling_copy(sib_rows).wait_recv()
 
-            far_work(t, w_own, g_own)
+            e, c = block_at(t)
+            far_work(e, c, w_own, g_own)
 
             @pl.when(t < 2 * nq)
             def _():
@@ -864,13 +917,13 @@
                 q = pair_q(i)
                 near_work(p, q, w_own, g_own)
 
-                @pl.when(p == 1)
+                @pl.when(t >= nq)
                 def _():
                     near_work(p, q, w_pair, g_pair)
 
-                    @pl.when(i >= nq)
-                    def _():
-                        edge_work(0, i - nq)
+                @pl.when(t >= near_fourth)
+                def _():
+                    edge_work(0, i - nq)
 
             @pl.when(has_pair)
             def _():
@@ -886,19 +939,15 @@
                 def _():
                     near_work(0, pair_q(lag), w_pair, g_pair)
 
-            @pl.when(jnp.logical_and(t >= 2 * nq, t < 3 * nq))
-            def _():
-                @pl.loop(0, 3)
-                def _(e):
-                    far_work(e * nq + t - 2 * nq, w_pair, g_pair)
-
-                @pl.when(t >= 2 * nq + kept)
+            @pl.when(t >= 2 * nq)
+            def _():
+                far_work(e, c, w_pair, g_pair)
+
+                @pl.when(t < 3 * nq)
                 def _():
-                    near_work(0, r_base + t - 2 * nq, w_pair, g_pair)
-
-            @pl.when(t >= 3 * nq)
-            def _():
-                far_work(t, w_pair, g_pair)
+                    @pl.loop(0, 2)
+                    def _(first):
+                        far_work(first, t - 2 * nq, w_pair, g_pair)
 
             @pl.when(t >= 3 * nq + kept)
             def _():
@@ -926,7 +975,7 @@
             has_pair = jnp.logical_and(turn >= 0, turn < 2 * nq)
             back = t - 2 * nq - 4
             has_back = jnp.logical_and(back >= 0, back < kept)
-            slot = jnp.where(t < 2 * nq + kept, t, t + nq - kept)
+            e, c = block_at(t)
             has_far = t < 2 * nq + 2 * kept
 
             @pl.when(turn == 0)
@@ -943,6 +992,12 @@
                 def _():
                     up_copy(g_pair.at[pair_q(turn)], 1, turn).start()
 
+                @pl.when(turn == nq - 1)
+                def _():
+                    @pl.loop(nq + kept, 2 * nq)
+                    def _(i):
+                        up_copy(g_src(pair_q(i)), 0, i).start()
+
             @pl.when(t == nq)
             def _():
                 sibling_copy(sib_rows).wait_recv()
@@ -957,12 +1012,12 @@
 
             @pl.when(has_far)
             def _():
-                wait_far(slot)
-                far_work(slot, w_own, g_own)
+                wait_far(t)
+                far_work(e, c, w_own, g_own)
 
             @pl.when(jnp.logical_and(has_far, t >= 2 * nq))
             def _():
-                far_work(slot, w_pair, g_pair)
+                far_work(e, c, w_pair, g_pair)
 
             @pl.when(t < 2 * nq)
             def _():
@@ -990,8 +1045,8 @@
             @pl.when(t >= 2 * nq)
             def _():
                 @pl.loop(0, 2)
-                def _(e):
-                    far_work(e * nq + t - 2 * nq, w_pair, g_pair)
+                def _(first):
+                    far_work(first, t - 2 * nq, w_pair, g_pair)
 
         share_part()
 
@@ -1108,7 +1163,7 @@
 def line_body(n_freq, chunk, nq, blocked, greens, weights):
     _, _, h, points = greens.shape
     n = 8
-    kept, late = 3 * nq // 8, 3
+    kept, late = 3 * nq // 8, 4
     stations = n * h
     dma = pltpu.SemaphoreType.DMA
     regular = pltpu.SemaphoreType.REGULAR
@@ -1140,7 +1195,7 @@
             dma((4 * nq,)), dma((4 * nq,)), dma((4 * nq + 1,)), dma((4 * nq,)), dma((2 * kept,)),
             dma((total // 2 - 1,)), dma((total // 2 - 1,)), dma((2,)),
             dma((2, total)), dma((2,)), dma((2,)), dma((2,)),
-            regular((2, 3)), regular((3,)),
+            regular((1,)), regular((2, 3)), regular((3,)),
         ],
         compiler_params=pltpu.CompilerParams(
             collective_id=0, has_side_effects=True, vmem_limit_bytes=60 * 1024 * 1024

time: 103 us -> 103 us (level)
  no operation moved by 1% of the time
where the time goes in v5:
time: 103 us
  Pallas kernels  102 us (99%)
    pallas_call x1, Pallas kernels, line_body(): pl.pallas_call(functools.partial(line_kernel, n_freq, h, stations, chunk,...  102 us

profile of v5, /device:TPU:0, one launch (start us, length us, event | category | flops | bytes accessed | tf_op | source)
XLA Modules:
  0.0 102.8 jit_solution(6372479275498559644)
XLA Ops:
  0.0 102.2 %shard_map.28 = f32[16,128]{1,0:T(8,128)S(1)} custom-call(bf16[2,2,256,2048]{3,2,1,0:T(8,128)(2,1)} %greens.1, bf16[2,2,256,2048]{3,2,1,0:T(8,128)(2,1)} %weights.1), custom_call_target="tpu_custom_call" | custom-call | tf_op jit(solution)/shard_map/pallas_call | solution.py:1174
  102.2 0.6 copy.4

commit v6 on v5

--- a/solution.py
+++ b/solution.py
@@ -441,10 +441,10 @@
 def line_kernel(
     n_freq, h, stations, chunk, nq, kept, late, blocked,
     greens, weights, out,
-    g_own, g_pair, near, far, w_own, w_pair, w_edge, folded, acc, part, side, sums, extras,
+    g_own, g_pair, near, far, w_own, w_pair, w_edge, folded, lent, acc, part, side, sums, extras,
     own_sem, w_own_sem, pair_send, pair_recv, wp_send, wp_recv, sib_sem, we_send, we_recv, we_sib,
     in_send, near_recv, far_recv, down_send, back_send, part_send, part_recv, side_sem,
-    extra_send, extra_recv, base_sem, fold_sem, reply_sem, hello_sem, pair_hello,
+    extra_send, extra_recv, base_sem, fold_sem, lend_sem, reply_sem, hello_sem, pair_hello,
 ):
     n = 8
     sub = chunk // LANES
@@ -519,22 +519,22 @@
         return greens.at[:, parity, :, columns(q)]
 
     def own_copy(q):
-        return pltpu.make_async_copy(g_src(q), g_own.at[q], own_sem.at[q])
+        return pltpu.make_async_copy(g_src(q), g_own.at[q], own_sem.at[0])
 
     def w_own_copy(j):
-        return pltpu.make_async_copy(w_src(parity, j, every_row), w_own.at[j], w_own_sem.at[j])
+        return pltpu.make_async_copy(w_src(parity, j, every_row), w_own.at[j], w_own_sem.at[0])
 
     def pair_copy(i):
         q = pair_q(i)
         return remote(
             greens.at[:, 1 - parity, :, columns(q)], g_pair.at[q],
-            pair_send.at[i], pair_recv.at[i], pair_dev,
+            pair_send.at[0], pair_recv.at[i], pair_dev,
         )
 
     def w_pair_copy(j):
         return remote(
             w_src(1 - parity, j, my_rows), w_pair.at[j, :, my_rows, :],
-            wp_send.at[j], wp_recv.at[j], pair_dev,
+            wp_send.at[0], wp_recv.at[0], pair_dev,
         )
 
     def sibling_copy(rows):
@@ -545,29 +545,33 @@
         part_of_w = w_edge.at[:, :, :, rows, :]
         return remote(part_of_w, part_of_w, we_sib.at[0], we_sib.at[1], core_dev)
 
+    def near_slot(p, i):
+        return p * (2 * nq - kept) + jnp.where(i < nq, i, i - kept)
+
+    def whole(ref, send_sem, recv_sem):
+        return remote(ref, ref, send_sem.at[0], recv_sem.at[0], pair_dev)
+
     def up_copy(src, p, i):
-        slot = p * 2 * nq + i
-        return remote(src, near.at[p, pair_q(i)], in_send.at[slot], near_recv.at[slot], in_dev)
+        return remote(src, near.at[p, pair_q(i)], in_send.at[0], near_recv.at[near_slot(p, i)], in_dev)
 
     def up_weights(src, b, p):
-        i = 2 * b + p
-        return remote(src, w_edge.at[b, p, :, my_rows, :], we_send.at[i], we_recv.at[i], in_dev)
+        return remote(src, w_edge.at[b, p, :, my_rows, :], we_send.at[0], we_recv.at[0], in_dev)
 
     def mid_copy(src, slot):
-        last = slot == steps - 1
-        land = jnp.where(jnp.logical_and(last, core == 0), steps, slot)
-        target = {"stn": me + inward, "pts": jnp.where(last, 1, core)}
-        return remote(src, far.at[land], in_send.at[slot], far_recv.at[land], target)
+        return remote(src, far.at[slot], in_send.at[0], far_recv.at[slot], in_dev)
+
+    def lend_copy():
+        src = near.at[1, pair_q(nq - 1)]
+        return remote(src, lent, lend_sem.at[0], lend_sem.at[1], core_dev)
 
     corner = 2 * nq - 2
 
     def down_copy(slot):
-        return remote(far.at[slot], far.at[slot], down_send.at[slot], far_recv.at[slot], out_dev)
+        return remote(far.at[slot], far.at[slot], down_send.at[0], far_recv.at[slot], out_dev)
 
     def back_copy(src, p, c):
         return remote(
-            src, near.at[p, (1 - hi) * nq + c], back_send.at[p * kept + c],
-            near_recv.at[p * 2 * nq + nq + c], out_dev,
+            src, near.at[p, r_base + c], back_send.at[0], near_recv.at[near_slot(p, c)], out_dev,
         )
 
     barrier = pltpu.get_barrier_semaphore()
@@ -654,13 +658,8 @@
 
     acc[...] = jnp.zeros_like(acc)
 
-    @pl.loop(0, 2 * nq)
-    def _(q):
-        own_copy(q).wait()
-
-    @pl.loop(0, n)
-    def _(j):
-        w_own_copy(j).wait()
+    pltpu.make_async_copy(g_own, g_own, own_sem.at[0]).wait()
+    pltpu.make_async_copy(w_own, w_own, w_own_sem.at[0]).wait()
 
     def product(w, gi, gj, s):
         lanes = slice(s * LANES, (s + 1) * LANES)
@@ -742,15 +741,15 @@
         remote(ref, ref, in_send.at[0], far_recv.at[t], in_dev).wait_recv()
 
     def wait_near(p, i):
-        slot = p * 2 * nq + i
         ref = near.at[p, pair_q(i)]
-        remote(ref, ref, in_send.at[slot], near_recv.at[slot], in_dev).wait_recv()
+        remote(ref, ref, in_send.at[0], near_recv.at[near_slot(p, i)], in_dev).wait_recv()
+
+    def wait_back(p, c):
+        ref = near.at[p, r_base + c]
+        remote(ref, ref, in_send.at[0], near_recv.at[near_slot(p, c)], in_dev).wait_recv()
 
     def wait_w_pair():
-        @pl.loop(0, n)
-        def _(j):
-            w_pair_copy(j).wait_recv()
-
+        whole(w_pair.at[:, :, my_rows, :], wp_send, wp_recv).wait_recv()
         sibling_copy(my_rows).start()
 
     def share_part():
@@ -774,7 +773,7 @@
 
     def part_copy(k, source):
         ref = part.at[source]
-        return remote(ref, ref, part_send.at[k - 1], part_recv.at[k - 1], at_rank(flipped(k)))
+        return remote(ref, ref, part_send.at[0], part_recv.at[0], at_rank(flipped(k)))
 
     my_group = (hi * 2 + parity) * n_freq + fq
     late_rows = late * sub
@@ -785,14 +784,14 @@
         def turned(v, bit):
             return 1 - v if k & bit else v
 
+        message = extras.at[core * 4 * n_freq + my_group]
         target_z = 2 * turned(hi, 8) + turned(lax.rem(z, 2), 4)
         target = {
             "stn": 2 * target_z + turned(parity, 2), "freq": turned(fq, 1),
             "pts": 1 - core if other else core,
         }
         return remote(
-            extras.at[core, my_group], extras.at[core, my_group],
-            extra_send.at[other, k], extra_recv.at[core], target,
+            message, message, extra_send.at[other], extra_recv.at[core], target,
         )
 
     def late_row(t):
@@ -801,9 +800,9 @@
     def finish():
         first = (r_base + nq - late) * sub
         for c in range(late_rows):
-            extras[core, my_group, c] = late_row(acc[first + c])
+            extras[core * 4 * n_freq + my_group, c] = late_row(acc[first + c])
         for s in range(sub):
-            extras[core, my_group, late_rows + s] = jnp.zeros((1, LANES), jnp.float32)
+            extras[core * 4 * n_freq + my_group, late_rows + s] = jnp.zeros((1, LANES), jnp.float32)
 
         @pl.when(core == 1)
         def _():
@@ -812,8 +811,8 @@
             wait_far(steps - 1)
             for s in range(sub):
                 c = late_rows - sub + s
-                extras[1, my_group, c] = late_row(acc[first + c] + unfold(1, steps - 1, s))
-                extras[1, my_group, late_rows + s] = late_row(unfold(0, steps, s))
+                extras[4 * n_freq + my_group, c] = late_row(acc[first + c] + unfold(1, steps - 1, s))
+                extras[4 * n_freq + my_group, late_rows + s] = late_row(unfold(0, steps, s))
 
         for k, other in sends:
             extra_copy(k, other).start()
@@ -886,19 +885,26 @@
             def _():
                 mid_copy(g_pair.at[pair_q(third)], 2 * nq + kept + third).start()
 
-            @pl.when(jnp.logical_and(fourth >= kept, fourth < nq))
+            @pl.when(jnp.logical_and(third == nq - 1, core == 0))
+            def _():
+                lend_copy().start()
+
+            @pl.when(jnp.logical_and(fourth >= kept, fourth < nq - 1 + core))
             def _():
                 mid_copy(near.at[1, pair_q(fourth)], 3 * nq + fourth).start()
 
+            @pl.when(jnp.logical_and(fourth == nq - 1, core == 1))
+            def _():
+                lend_copy().wait_recv()
+                mid_copy(lent, steps).start()
+
             @pl.when(t == nq + 2)
             def _():
                 sibling_copy(sib_rows).wait_recv()
 
             @pl.when(t == near_second)
             def _():
-                for r in range(4):
-                    part_of_w = w_edge.at[r // 2, r % 2, :, my_rows, :]
-                    up_weights(part_of_w, r // 2, r % 2).wait_recv()
+                whole(w_edge.at[:, :, :, my_rows, :], we_send, we_recv).wait_recv()
                 edge_sibling_copy(my_rows).start()
 
             @pl.when(t == near_second + 2)
@@ -1004,11 +1010,11 @@
 
             @pl.when(t < kept)
             def _():
-                wait_near(0, nq + t)
+                wait_back(0, t)
 
             @pl.when(has_back)
             def _():
-                wait_near(1, nq + back)
+                wait_back(1, back)
 
             @pl.when(has_far)
             def _():
@@ -1050,9 +1056,8 @@
 
         share_part()
 
-    @pl.loop(1, total // 2)
-    def _(k):
-        part_copy(k, flipped(k)).wait_recv()
+    parts = part.at[pl.ds(0, total // 2 - 1)]
+    whole(parts, part_send, part_recv).wait_recv()
 
     base = hi * (total // 2)
     mine = part[base]
@@ -1070,62 +1075,43 @@
     base_copy = remote(sums.at[core], sums.at[core], base_sem.at[0], base_sem.at[1], core_dev)
     base_copy.start()
 
-    @pl.loop(0, 2 * nq)
-    def _(i):
-        pair_copy(i).wait_send()
-
-    @pl.loop(0, n)
-    def _(j):
-        w_pair_copy(j).wait_send()
-
+    whole(g_pair, pair_send, pair_recv).wait_send()
+    whole(w_pair.at[:, :, my_rows, :], wp_send, wp_recv).wait_send()
     sibling_copy(my_rows).wait_send()
-
-    @pl.loop(1, total // 2)
-    def _(k):
-        part_copy(k, rank).wait_send()
+    whole(parts, part_send, part_recv).wait_send()
+
+    def sent(count, send_sem):
+        whole(far.at[pl.ds(0, count)], send_sem, far_recv).wait_send()
 
     @pl.when(inner)
     def _():
-        @pl.loop(0, steps)
-        def _(t):
-            mid_copy(far.at[0], t).wait_send()
-
-            @pl.when(passed_down(t))
-            def _():
-                down_copy(t).wait_send()
-
-        @pl.loop(0, 2 * kept)
-        def _(i):
-            back_copy(g_own.at[0], i // kept, lax.rem(i, kept)).wait_send()
-
-        for k, other in sends:
-            extra_copy(k, other).wait_send()
-
+        sent(2 * nq + 2 * kept, down_send)
+        sent(2 * kept, back_send)
         edge_sibling_copy(my_rows).wait_send()
+        for other in range(2):
+            ref = extras.at[pl.ds(0, total - 1 + other)]
+            remote(ref, ref, extra_send.at[other], extra_recv.at[0], core_dev).wait_send()
 
         @pl.when(core == 0)
         def _():
+            sent(steps - 1, in_send)
             fold_copy().wait_send()
+            lend_copy().wait_send()
+
+        @pl.when(core == 1)
+        def _():
+            sent(steps + 1, in_send)
 
     @pl.when(outer)
     def _():
-        @pl.loop(0, 4 * nq)
-        def _(s):
-            i = lax.rem(s, 2 * nq)
-
-            @pl.when(jnp.logical_or(i < nq, i >= nq + kept))
-            def _():
-                up_copy(g_own.at[0], s // (2 * nq), i).wait_send()
-
-        for r in range(4):
-            part_of_w = w_edge.at[r // 2, r % 2, :, my_rows, :]
-            up_weights(part_of_w, r // 2, r % 2).wait_send()
+        sent(steps - 2 * kept, in_send)
+        whole(w_edge.at[:, :, :, my_rows, :], we_send, we_recv).wait_send()
 
     side_copy(hi).wait_send()
 
     def wait_extras(which, groups):
-        ref = extras.at[which, pl.ds(0, groups)]
-        remote(ref, ref, extra_send.at[0, 0], extra_recv.at[which], core_dev).wait_recv()
+        ref = extras.at[pl.ds(which * 4 * n_freq, groups)]
+        remote(ref, ref, extra_send.at[0], extra_recv.at[which], core_dev).wait_recv()
 
     @pl.when(inner)
     def _():
@@ -1142,19 +1128,20 @@
     remote(sum_ref, sum_ref, base_sem.at[0], base_sem.at[1], core_dev).wait_recv()
 
     def late_sum(which, low, c):
-        row = extras[which, low * 2 * n_freq, c]
+        first = (2 * which + low) * 2 * n_freq
+        row = extras[first, c]
         for g in range(1, 2 * n_freq):
-            row = row + extras[which, low * 2 * n_freq + g, c]
+            row = row + extras[first + g, c]
         return row
 
     for which in range(2):
         for low in range(2):
-            for c in range(late_rows):
-                row = late_sum(which, low, c)
-                if which == 0 and c >= late_rows - sub:
-                    row = row + late_sum(1, low, c + sub)
-                at = ((1 - low) * nq + nq - late) * sub + c
-                sums[which, at:at + 1, :] += row
+            gathered = [late_sum(which, low, c) for c in range(late_rows)]
+            if which == 0:
+                for s in range(sub):
+                    gathered[late_rows - sub + s] += late_sum(1, low, late_rows + s)
+            at = ((1 - low) * nq + nq - late) * sub
+            sums[which, at:at + late_rows, :] += jnp.concatenate(gathered, axis=0)
 
     largest = jnp.max(jnp.maximum(jnp.abs(sums[0]), jnp.abs(sums[1])), keepdims=True)
     out[...] = sums[core] / (largest + 1e-6)
@@ -1166,6 +1153,7 @@
     kept, late = 3 * nq // 8, 4
     stations = n * h
     dma = pltpu.SemaphoreType.DMA
+    one, two = dma((1,)), dma((2,))
     regular = pltpu.SemaphoreType.REGULAR
     bf16, f32 = jnp.bfloat16, jnp.float32
     rows = points // LANES
@@ -1185,16 +1173,17 @@
             pltpu.VMEM((n, 2, h, h), bf16),
             pltpu.VMEM((2, 2, 2, h, h), bf16),
             pltpu.VMEM((2, 2, h, chunk), f32),
+            pltpu.VMEM((2, h, chunk), bf16),
             pltpu.VMEM((rows, 8, LANES), f32),
             pltpu.VMEM((total, rows, LANES), f32),
             pltpu.VMEM((2, rows, LANES), f32),
             pltpu.VMEM((2, rows, LANES), f32),
-            pltpu.VMEM((2, 4 * n_freq, late_rows + chunk // LANES, 1, LANES), f32),
-            dma((2 * nq,)), dma((n,)), dma((2 * nq,)), dma((2 * nq,)), dma((n,)), dma((n,)), dma((2,)),
-            dma((4,)), dma((4,)), dma((2,)),
-            dma((4 * nq,)), dma((4 * nq,)), dma((4 * nq + 1,)), dma((4 * nq,)), dma((2 * kept,)),
-            dma((total // 2 - 1,)), dma((total // 2 - 1,)), dma((2,)),
-            dma((2, total)), dma((2,)), dma((2,)), dma((2,)),
+            pltpu.VMEM((8 * n_freq, late_rows + chunk // LANES, 1, LANES), f32),
+            one, one, one, dma((2 * nq,)), one, one, two,
+            one, one, two,
+            one, dma((4 * nq - 2 * kept,)), dma((4 * nq + 1,)), one, one,
+            one, one, two,
+            two, two, two, two, two,
             regular((1,)), regular((2, 3)), regular((3,)),
         ],
         compiler_params=pltpu.CompilerParams(

time: 103 us -> 101 us (0.981)
    pallas_call x1, Pallas kernels: 102 us -> 101 us  [line_body(): pl.pallas_call(functools.partial(line_kernel, n_freq, h, stations, chunk,...]
where the time goes in v6:
time: 101 us
  Pallas kernels  101 us (100%)
    pallas_call x1, Pallas kernels, line_body(): pl.pallas_call(functools.partial(line_kernel, n_freq, h, stations, chunk,...  101 us

profile of v6, /device:TPU:0, one launch (start us, length us, event | category | flops | bytes accessed | tf_op | source)
XLA Modules:
  0.0 101.3 jit_solution(6725451425630733722)
XLA Ops:
  0.0 100.7 %shard_map.28 = f32[16,128]{1,0:T(8,128)S(1)} custom-call(bf16[2,2,256,2048]{3,2,1,0:T(8,128)(2,1)} %greens.1, bf16[2,2,256,2048]{3,2,1,0:T(8,128)(2,1)} %weights.1), custom_call_target="tpu_custom_call" | custom-call | tf_op jit(solution)/shard_map/pallas_call | solution.py:1162
  100.7 0.6 copy.4

commit v7 on v6

--- a/solution.py
+++ b/solution.py
@@ -402,7 +402,7 @@
     blocked = h % LANES != 0
     if blocked:
         weights = weights.reshape(2, weights.shape[1], h, n, h).swapaxes(2, 3)
-    if side_len == 2 and nq >= 4:
+    if side_len == 2 and nq >= 8 and nq % 2 == 0:
         return line_body(n_freq, chunk, nq, blocked, greens, weights)
     dma = pltpu.SemaphoreType.DMA
     bf16, f32 = jnp.bfloat16, jnp.float32
@@ -528,7 +528,7 @@
         q = pair_q(i)
         return remote(
             greens.at[:, 1 - parity, :, columns(q)], g_pair.at[q],
-            pair_send.at[0], pair_recv.at[i], pair_dev,
+            pair_send.at[0], pair_recv.at[i // 2], pair_dev,
         )
 
     def w_pair_copy(j):
@@ -545,8 +545,16 @@
         part_of_w = w_edge.at[:, :, :, rows, :]
         return remote(part_of_w, part_of_w, we_sib.at[0], we_sib.at[1], core_dev)
 
+    first_groups = nq // 2 + (nq - kept + 1) // 2
+    back_group = first_groups + nq // 2 + nq - kept
+    singles = 2 * nq + 2 * kept
+
     def near_slot(p, i):
-        return p * (2 * nq - kept) + jnp.where(i < nq, i, i - kept)
+        m = i - nq - kept
+        return p * first_groups + jnp.where(i < nq, i // 2, nq // 2 + jnp.where(p == 0, m // 2, m))
+
+    def far_slot(slot):
+        return jnp.where(slot < singles, slot // 2, slot - singles // 2)
 
     def whole(ref, send_sem, recv_sem):
         return remote(ref, ref, send_sem.at[0], recv_sem.at[0], pair_dev)
@@ -558,7 +566,7 @@
         return remote(src, w_edge.at[b, p, :, my_rows, :], we_send.at[0], we_recv.at[0], in_dev)
 
     def mid_copy(src, slot):
-        return remote(src, far.at[slot], in_send.at[0], far_recv.at[slot], in_dev)
+        return remote(src, far.at[slot], in_send.at[0], far_recv.at[far_slot(slot)], in_dev)
 
     def lend_copy():
         src = near.at[1, pair_q(nq - 1)]
@@ -567,11 +575,11 @@
     corner = 2 * nq - 2
 
     def down_copy(slot):
-        return remote(far.at[slot], far.at[slot], down_send.at[0], far_recv.at[slot], out_dev)
+        return remote(far.at[slot], far.at[slot], down_send.at[0], far_recv.at[far_slot(slot)], out_dev)
 
     def back_copy(src, p, c):
         return remote(
-            src, near.at[p, r_base + c], back_send.at[0], near_recv.at[near_slot(p, c)], out_dev,
+            src, near.at[p, r_base + c], back_send.at[0], near_recv.at[back_group + p], out_dev,
         )
 
     barrier = pltpu.get_barrier_semaphore()
@@ -640,17 +648,17 @@
         for b in range(2):
             up_weights(w_src(parity, far_block(2 + b), my_rows), b, 0).start()
 
-    @pl.loop(0, 3)
+    @pl.loop(0, 2)
     def _(r):
-        along_z(hello_sem.at[0, r], hello_sem.at[1, r])
+        along_z(hello_sem.at[0], hello_sem.at[1])
 
         @pl.when(up)
         def _():
-            pl.semaphore_wait(hello_sem.at[0, r], 1)
+            pl.semaphore_wait(hello_sem.at[0], 1)
 
         @pl.when(down)
         def _():
-            pl.semaphore_wait(hello_sem.at[1, r], 1)
+            pl.semaphore_wait(hello_sem.at[1], 1)
 
     for i, device in enumerate((pair_dev, freq_dev, core_dev)):
         greet(pair_hello.at[i], device)
@@ -736,17 +744,41 @@
     def passed_down(t):
         return t < 2 * nq + 2 * kept
 
+    def wait_blocks(count, recv_sem):
+        ref = far.at[pl.ds(0, count)]
+        remote(ref, ref, in_send.at[0], recv_sem, in_dev).wait_recv()
+
     def wait_far(t):
-        ref = far.at[t]
-        remote(ref, ref, in_send.at[0], far_recv.at[t], in_dev).wait_recv()
+        @pl.when(jnp.logical_and(t < singles, lax.rem(t, 2) == 0))
+        def _():
+            wait_blocks(2, far_recv.at[t // 2])
+
+        @pl.when(t >= singles)
+        def _():
+            wait_blocks(1, far_recv.at[t - singles // 2])
+
+    def wait_pair(i):
+        @pl.when(lax.rem(i, 2) == 0)
+        def _():
+            wait_blocks(2, pair_recv.at[i // 2])
 
     def wait_near(p, i):
-        ref = near.at[p, pair_q(i)]
-        remote(ref, ref, in_send.at[0], near_recv.at[near_slot(p, i)], in_dev).wait_recv()
-
-    def wait_back(p, c):
-        ref = near.at[p, r_base + c]
-        remote(ref, ref, in_send.at[0], near_recv.at[near_slot(p, c)], in_dev).wait_recv()
+        m = jnp.where(i < nq, i, i - nq - kept)
+        even = lax.rem(m, 2) == 0
+        alone = jnp.logical_and(i >= nq, p == 1)
+        two = even & jnp.logical_not(alone) & (i < 2 * nq - 1)
+        lone = jnp.logical_or(alone, even & (i == 2 * nq - 1))
+
+        @pl.when(two)
+        def _():
+            wait_blocks(2, near_recv.at[near_slot(p, i)])
+
+        @pl.when(lone)
+        def _():
+            wait_blocks(1, near_recv.at[near_slot(p, i)])
+
+    def wait_back(p):
+        wait_blocks(kept, near_recv.at[back_group + p])
 
     def wait_w_pair():
         whole(w_pair.at[:, :, my_rows, :], wp_send, wp_recv).wait_recv()
@@ -807,8 +839,8 @@
         @pl.when(core == 1)
         def _():
             fold_copy().wait_recv()
-            wait_far(steps)
-            wait_far(steps - 1)
+            wait_blocks(1, far_recv.at[steps - singles // 2])
+            wait_blocks(1, far_recv.at[steps - 1 - singles // 2])
             for s in range(sub):
                 c = late_rows - sub + s
                 extras[4 * n_freq + my_group, c] = late_row(acc[first + c] + unfold(1, steps - 1, s))
@@ -862,7 +894,7 @@
 
             @pl.when(has_pair)
             def _():
-                pair_copy(turn).wait_recv()
+                wait_pair(turn)
 
                 @pl.when(turn < kept)
                 def _():
@@ -992,7 +1024,7 @@
 
             @pl.when(has_pair)
             def _():
-                pair_copy(turn).wait_recv()
+                wait_pair(turn)
 
                 @pl.when(jnp.logical_or(turn < nq, turn >= nq + kept))
                 def _():
@@ -1008,13 +1040,13 @@
             def _():
                 sibling_copy(sib_rows).wait_recv()
 
-            @pl.when(t < kept)
-            def _():
-                wait_back(0, t)
-
-            @pl.when(has_back)
-            def _():
-                wait_back(1, back)
+            @pl.when(t == 0)
+            def _():
+                wait_back(0)
+
+            @pl.when(back == 0)
+            def _():
+                wait_back(1)
 
             @pl.when(has_far)
             def _():
@@ -1150,10 +1182,11 @@
 def line_body(n_freq, chunk, nq, blocked, greens, weights):
     _, _, h, points = greens.shape
     n = 8
-    kept, late = 3 * nq // 8, 4
+    kept, late = 3 * nq // 8, 3
     stations = n * h
     dma = pltpu.SemaphoreType.DMA
     one, two = dma((1,)), dma((2,))
+    near_groups = nq + (nq - kept + 1) // 2 + nq - kept + 2
     regular = pltpu.SemaphoreType.REGULAR
     bf16, f32 = jnp.bfloat16, jnp.float32
     rows = points // LANES
@@ -1179,12 +1212,12 @@
             pltpu.VMEM((2, rows, LANES), f32),
             pltpu.VMEM((2, rows, LANES), f32),
             pltpu.VMEM((8 * n_freq, late_rows + chunk // LANES, 1, LANES), f32),
-            one, one, one, dma((2 * nq,)), one, one, two,
+            one, one, one, dma((nq,)), one, one, two,
             one, one, two,
-            one, dma((4 * nq - 2 * kept,)), dma((4 * nq + 1,)), one, one,
+            one, dma((near_groups,)), dma((3 * nq + 1 - kept,)), one, one,
             one, one, two,
             two, two, two, two, two,
-            regular((1,)), regular((2, 3)), regular((3,)),
+            regular((1,)), regular((2,)), regular((3,)),
         ],
         compiler_params=pltpu.CompilerParams(
             collective_id=0, has_side_effects=True, vmem_limit_bytes=60 * 1024 * 1024

time: 101 us -> 101 us (level)
  no operation moved by 1% of the time
where the time goes in v7:
time: 101 us
  Pallas kernels  100 us (99%)
    pallas_call x1, Pallas kernels, line_body(): pl.pallas_call(functools.partial(line_kernel, n_freq, h, stations, chunk,...  100 us

profile of v7, /device:TPU:0, one launch (start us, length us, event | category | flops | bytes accessed | tf_op | source)
XLA Modules:
  0.0 101.0 jit_solution(14485937814160632222)
XLA Ops:
  0.0 100.4 %shard_map.28 = f32[16,128]{1,0:T(8,128)S(1)} custom-call(bf16[2,2,256,2048]{3,2,1,0:T(8,128)(2,1)} %greens.1, bf16[2,2,256,2048]{3,2,1,0:T(8,128)(2,1)} %weights.1), custom_call_target="tpu_custom_call" | custom-call | tf_op jit(solution)/shard_map/pallas_call | solution.py:1195
  100.4 0.6 copy.4

commit v8 on v7

--- a/solution.py
+++ b/solution.py
@@ -435,7 +435,7 @@
     return out.reshape(points)
 
 
-FAR_FIRST = (11, 9, 10, 8, 15, 7, 13, 14, 5, 6, 12, 4, 3, 1, 2, 0)
+FAR_FIRST = (11, 9, 10, 8, 7, 5, 6, 4, 15, 13, 14, 12, 3, 1, 2, 0)
 
 
 def line_kernel(

time: 101 us -> 101 us (level)
  no operation moved by 1% of the time
where the time goes in v8:
time: 101 us
  Pallas kernels  100 us (99%)
    pallas_call x1, Pallas kernels, line_body(): pl.pallas_call(functools.partial(line_kernel, n_freq, h, stations, chunk,...  100 us

profile of v8, /device:TPU:0, one launch (start us, length us, event | category | flops | bytes accessed | tf_op | source)
XLA Modules:
  0.0 101.0 jit_solution(12179949300526168109)
XLA Ops:
  0.0 100.4 %shard_map.28 = f32[16,128]{1,0:T(8,128)S(1)} custom-call(bf16[2,2,256,2048]{3,2,1,0:T(8,128)(2,1)} %greens.1, bf16[2,2,256,2048]{3,2,1,0:T(8,128)(2,1)} %weights.1), custom_call_target="tpu_custom_call" | custom-call | tf_op jit(solution)/shard_map/pallas_call | solution.py:1195
  100.4 0.6 copy.4
